TPU v7x, 128 devices: a whole 4x4x4 slice. The times are simulated.
128 devices in a mesh: seq: 64 (over z, x, y), batch: 2 (over core).
Axes of the slice: x: 4, y: 4, z: 4, core: 2. Of those that a mesh axis runs over, the one named last changes fastest.
Arguments:
- inputs: bfloat16 [2, 8192, 2048], P('batch', 'seq'), may hold values from -6 to 6
- cotangent: bfloat16 [2, 8192, 1024], P('batch', 'seq'), may hold values from -48 to 48
- w_query: bfloat16 [2048, 128], replicated, may hold values from -0.125 to 0.125
- w_key: bfloat16 [2048, 128], replicated, may hold values from -0.125 to 0.125
- w_value: bfloat16 [2048, 1024], replicated, may hold values from -0.125 to 0.125
Outputs:
- grad_inputs: bfloat16 [2, 8192, 2048], P('batch', 'seq')
- grad_w_query: float32 [2048, 128], P(('seq', 'batch'))
- grad_w_key: float32 [2048, 128], P(('seq', 'batch'))
- grad_w_value: float32 [2048, 1024], P(('seq', 'batch'))
All inputs are finite; a program needn't handle non-finite values.
Results may differ from a plain program's by a relative error of at most 0.006.
Values sent between devices are 32-bit elements; how exact they have to be, the bound alone decides.
A program may use at most 128 MiB of HBM per device.

v0:
```python
import functools
import math

import jax
import jax.numpy as jnp
import numpy as np
from jax import lax
from jax.experimental import pallas as pl
from jax.experimental.pallas import tpu as pltpu
from jax.sharding import PartitionSpec as P

H = 8
DK = 16
DV = 128
AUX = 16
MESH = pl.DeviceIdType.MESH
BF = jnp.bfloat16
F32 = jnp.float32


def group(kind, outer, inner):
    seq = lax.axis_index("seq")
    core = lax.axis_index("batch")
    high = seq // inner
    low = seq % inner
    if kind == "seq":
        return outer * inner, seq, lambda j: (j, core)
    if kind == "plane":
        return inner * 2, low * 2 + core, lambda j: (high * inner + j // 2, j % 2)
    if kind == "line":
        return outer, high, lambda j: (j * inner + low, core)
    if kind == "chips":
        return inner, low, lambda j: (high * inner + j, core)
    return 2, core, lambda j: (seq, j)


def greet(groups):
    barrier = pltpu.get_barrier_semaphore()
    total = 0
    for size, me, where in groups:
        for k in range(1, size):
            pl.semaphore_signal(
                barrier, inc=1, device_id=where((me + k) % size), device_id_type=MESH
            )
        total += size - 1
    pl.semaphore_wait(barrier, total)


def push(src, dst, send, recv, device):
    copy = pltpu.make_async_remote_copy(
        src_ref=src,
        dst_ref=dst,
        send_sem=send,
        recv_sem=recv,
        device_id=device,
        device_id_type=MESH,
    )
    copy.start()
    return copy


VMEM = pl.BlockSpec(memory_space=pltpu.VMEM)
HBM = pl.BlockSpec(memory_space=pl.ANY)


def sems(*sizes):
    return pltpu.SemaphoreType.DMA(sizes)


def params(number):
    return pltpu.CompilerParams(
        collective_id=number, has_side_effects=True, vmem_limit_bytes=60 << 20
    )


def dot(left, right, dims):
    return lax.dot_general(left, right, ((dims[:1], dims[1:]), ((), ())), preferred_element_type=F32)


def halves(a):
    high = a.astype(BF)
    return high, (a - high.astype(F32)).astype(BF)


def dot2(pair, right, dims):
    return dot(pair[0], right, dims) + dot(pair[1], right, dims)


def dot2r(left, pair, dims):
    return dot(left, pair[0], dims) + dot(left, pair[1], dims)


def dot3(lefts, rights, dims):
    return (
        dot(lefts[0], rights[0], dims)
        + dot(lefts[0], rights[1], dims)
        + dot(lefts[1], rights[0], dims)
    )


def coefs():
    table = np.where(np.eye(DK) > 0, 1.0 / math.sqrt(2.0), 1.0).astype(np.float32)
    table = table * (np.arange(DK)[:, None] <= np.arange(DK)[None, :])
    half = DK // 2
    rows = np.concatenate([table[:half].reshape(-1), table[half:, half:].reshape(-1)])
    return np.ascontiguousarray(np.broadcast_to(rows[:, None], (rows.size, 128)))


def phi(u, coef):
    half = DK // 2
    lanes = u.shape[1]
    pieces = []
    for i in range(DK):
        low = u if i < half else u[half:]
        pieces.append(u[i : i + 1] * low)
    pairs = jnp.concatenate(pieces, 0) * coef
    first = (lax.broadcasted_iota(jnp.int32, (AUX, lanes), 0) == 0).astype(F32)
    return jnp.concatenate([pairs, u, first], 0)


def pull(u, grad, coef):
    half = DK // 2
    pairs = grad[: coef.shape[0]] * coef
    linear = grad[coef.shape[0] : coef.shape[0] + DK]
    rows = lax.broadcasted_iota(jnp.int32, u.shape, 0)
    total = linear
    lower = jnp.zeros_like(u[half:])
    at = 0
    for i in range(DK):
        if i < half:
            piece = pairs[at : at + DK]
            at += DK
            total = total + piece * u[i : i + 1]
            mine = jnp.sum(piece * u, 0, keepdims=True)
        else:
            piece = pairs[at : at + half]
            at += half
            lower = lower + piece * u[i : i + 1]
            mine = jnp.sum(piece * u[half:], 0, keepdims=True)
        total = total + jnp.where(rows == i, mine, 0.0)
    return total + jnp.concatenate([jnp.zeros_like(lower), lower], 0)


def attention_kernel(
    wide, outer, inner, r_ref, c_ref, x_ref, got_ref, xb_ref,
    o_ref, fq_ref, fk_ref, va_ref, ah, al, gh, gl, nh, nl, st_ref, gi_ref, pg_ref,
    send_i, recv_i, send_x, recv_x, send_r, recv_r,
):
    blocks, _, tokens = r_ref.shape
    size, me, where = group("seq", outer, inner)
    chips, low, chip = group("chips", outer, inner)
    _, core, sibling = group("pair", outer, inner)
    rows = st_ref.shape[2] // outer
    for j in range(inner):
        for z in range(outer):
            at = (z * inner + j) * rows
            st_ref[j, :, z * rows : (z + 1) * rows] = x_ref[:, at : at + rows].astype(F32)
    greet([(size, me, where), (chips, low, chip), (2, core, sibling)])
    inside = []
    for k in range(1, chips):
        peer = (low + k) % chips
        inside.append(
            push(st_ref.at[peer], gi_ref.at[low], send_i.at[k], recv_i.at[k], chip(peer))
        )
    gi_ref[low] = st_ref[low]
    length = 2 * tokens
    chunks = blocks // 2
    feats = fq_ref.shape[1]
    coef = jnp.concatenate([c_ref[...]] * (length // 128), 1)
    causal = lax.broadcasted_iota(jnp.int32, (length, length), 0) <= lax.broadcasted_iota(
        jnp.int32, (length, length), 1
    )
    aux_row = lax.broadcasted_iota(jnp.int32, (AUX, length), 0) == 0

    def block(c):
        return jnp.concatenate([r_ref[2 * c], r_ref[2 * c + 1]], 1)

    def store(c, start, rows):
        size = rows.shape[0]
        o_ref[2 * c, start : start + size, :] = rows[:, :tokens]
        o_ref[2 * c + 1, start : start + size, :] = rows[:, tokens:]

    def forward(c, state):
        both = block(c)
        uq = both[:DK] * 0.5
        uk = both[DK : 2 * DK] * 0.5
        val = both[2 * DK : 2 * DK + wide]
        up = both[2 * DK + wide :]
        fq = phi(uq, coef).astype(BF)
        fk = phi(uk, coef).astype(BF)
        va = jnp.concatenate([val, aux_row.astype(F32)], 0).astype(BF)
        fq_ref[c] = fq
        fk_ref[c] = fk
        va_ref[c] = va
        attn = halves(jnp.where(causal, dot(fk, fq, (0, 0)), 0.0))
        ah[c] = attn[0]
        al[c] = attn[1]
        held = halves(state)
        top = dot2r(va, attn, (1, 0)) + dot2(held, fq, (1, 0))
        scale = 1.0 / top[wide : wide + 1]
        numer = up * scale
        denom = -jnp.sum(numer * top[:wide], 0, keepdims=True) * scale
        gn = halves(jnp.concatenate([numer, jnp.where(aux_row, denom, 0.0)], 0))
        nh[c] = gn[0]
        nl[c] = gn[1]
        ga = halves(jnp.where(causal, dot2r(va, gn, (0, 0)), 0.0))
        gh[c] = ga[0]
        gl[c] = ga[1]
        gfq = dot2r(fk, ga, (1, 0)) + dot3(held, gn, (0, 0))
        store(c, 0, pull(uq, gfq, coef) * 0.5)
        return state + dot(va, fk, (1, 1))

    zero = jnp.zeros((wide + AUX, feats), F32)
    lax.fori_loop(0, chunks, forward, zero)

    def backward(step, state):
        c = chunks - 1 - step
        uk = block(c)[DK : 2 * DK] * 0.5
        fq, fk, va = fq_ref[c], fk_ref[c], va_ref[c]
        attn = (ah[c], al[c])
        ga = (gh[c], gl[c])
        gn = (nh[c], nl[c])
        held = halves(state)
        gv = dot3(gn, attn, (1, 1)) + dot2(held, fk, (1, 0))
        store(c, 2 * DK, gv[:wide])
        gfk = dot2r(fq, ga, (1, 1)) + dot2(held, va, (0, 0))
        store(c, DK, pull(uk, gfk, coef) * 0.5)
        for t in range(2):
            peer = 2 * c + t

            @pl.when(peer != me)
            def _():
                push(o_ref.at[peer], got_ref.at[me], send_r.at[peer], recv_r.at[me], where(peer))

        return state + dot2(gn, fq, (1, 1))

    lax.fori_loop(0, chunks, backward, zero)
    got_ref[me] = o_ref[me]
    for copy in inside:
        copy.wait()
    pair = push(gi_ref, pg_ref, send_x.at[0], recv_x.at[0], sibling(1 - core))
    for j in range(inner):
        xb_ref[2 * j + core] = gi_ref[j].astype(BF)
    pair.wait()
    for j in range(inner):
        xb_ref[2 * j + 1 - core] = pg_ref[j].astype(BF)
    for k in range(1, size):
        peer = (me + k) % size
        pltpu.make_async_remote_copy(
            src_ref=o_ref.at[peer],
            dst_ref=got_ref.at[peer],
            send_sem=send_r.at[peer],
            recv_sem=recv_r.at[peer],
            device_id=where(peer),
            device_id_type=MESH,
        ).wait()


def attention(received, tokens_in, wide, outer, inner):
    blocks, _, tokens = received.shape
    coef = coefs()
    feats = coef.shape[0] + DK + AUX
    chunks, length = blocks // 2, 2 * tokens
    width = tokens_in.shape[1] // inner
    square = pltpu.VMEM((chunks, length, length), BF)
    grads = pltpu.VMEM((chunks, wide + AUX, length), BF)
    feat = pltpu.VMEM((chunks, feats, length), BF)
    result = (blocks, 2 * DK + wide, tokens)
    group_in = pltpu.VMEM((inner, tokens, width), F32)
    scratch = [pltpu.VMEM(result, F32), feat, feat, grads, square, square, square, square]
    scratch += [grads, grads, group_in, group_in, group_in]
    scratch += [sems(inner)] * 2 + [sems(1)] * 2 + [sems(blocks)] * 2
    return pl.pallas_call(
        functools.partial(attention_kernel, wide, outer, inner),
        out_shape=[
            jax.ShapeDtypeStruct(result, F32),
            jax.ShapeDtypeStruct((2 * inner, tokens, width), BF),
        ],
        in_specs=[VMEM] * 3,
        out_specs=[VMEM] * 2,
        scratch_shapes=scratch,
        compiler_params=params(1),
    )(received, jnp.asarray(coef), tokens_in)


def front_kernel(
    outer, inner, x_ref, c_ref, wq_hbm, wk_hbm, wv_hbm, out_ref,
    wq_ref, wk_ref, wv_ref, own_ref, up_ref, load, send_u, recv_u, send_p, recv_p,
):
    loads = []
    for n, (src, dst) in enumerate(((wq_hbm, wq_ref), (wk_hbm, wk_ref), (wv_hbm, wv_ref))):
        copy = pltpu.make_async_copy(src, dst, load.at[n])
        copy.start()
        loads.append(copy)
    size, me, where = group("seq", outer, inner)
    split = size // H
    wide = DV // split
    cut = 2 * DK + wide
    for h in range(H):
        flat = c_ref[:, h * DV : (h + 1) * DV].astype(F32).T
        for n in range(split):
            up_ref[h * split + n] = flat[n * wide : (n + 1) * wide]
    greet([(size, me, where)])
    copies = []
    for k in range(1, size):
        peer = (me + k) % size
        dst = out_ref.at[me, pl.ds(cut, wide)]
        copies.append(push(up_ref.at[peer], dst, send_u.at[k], recv_u.at[k], where(peer)))
    x = x_ref[...]
    for n, (w_ref, copy) in enumerate(zip((wq_ref, wk_ref), loads)):
        copy.wait()
        flat = dot(x, w_ref[...], (1, 0)).T
        for s in range(size):
            at = (s // split) * DK
            own_ref[s, n * DK : (n + 1) * DK, :] = flat[at : at + DK]
    loads[2].wait()
    for h in range(H):
        flat = dot(x, wv_ref[:, h * DV : (h + 1) * DV], (1, 0)).astype(BF).astype(F32).T
        for n in range(split):
            own_ref[h * split + n, 2 * DK :, :] = flat[n * wide : (n + 1) * wide]
    for k in range(1, size):
        peer = (me + k) % size
        dst = out_ref.at[me, pl.ds(0, cut)]
        copies.append(push(own_ref.at[peer], dst, send_p.at[k], recv_p.at[k], where(peer)))
    out_ref[me, :cut, :] = own_ref[me]
    out_ref[me, cut:, :] = up_ref[me]
    for copy in copies:
        copy.wait()


def front(tokens, upstream, weights, outer, inner):
    seqs = outer * inner
    length = tokens.shape[0]
    wide = DV * H // seqs
    cut = 2 * DK + wide
    scratch = [pltpu.VMEM(w.shape, w.dtype) for w in weights]
    scratch += [pltpu.VMEM((seqs, cut, length), F32), pltpu.VMEM((seqs, wide, length), F32)]
    return pl.pallas_call(
        functools.partial(front_kernel, outer, inner),
        out_shape=jax.ShapeDtypeStruct((seqs, cut + wide, length), F32),
        in_specs=[VMEM] * 2 + [HBM] * 3,
        out_specs=VMEM,
        scratch_shapes=scratch + [sems(3)] + [sems(seqs)] * 4,
        compiler_params=params(0),
    )(tokens, upstream, *weights)


def tail_kernel(
    outer, inner, pieces, g_ref, xb_ref, wq_hbm, wk_hbm, wv_hbm, gi_ref, oq_ref, ok_ref, ov_ref,
    wq_ref, wk_ref, wv_ref, jt_ref, jb_ref, gj_ref, ls_ref, lr_ref, fs_ref, os_ref, o_ref,
    load, send_j, recv_j, send_l, recv_l, send_o, recv_o,
):
    loads = []
    for n, (src, dst) in enumerate(((wq_hbm, wq_ref), (wk_hbm, wk_ref), (wv_hbm, wv_ref))):
        copy = pltpu.make_async_copy(src, dst, load.at[n])
        copy.start()
        loads.append(copy)
    plane, mine, where = group("plane", outer, inner)
    lines, high, along = group("line", outer, inner)
    _, core, sibling = group("pair", outer, inner)
    greet([(plane, mine, where), (lines, high, along), (2, core, sibling)])
    other = 1 - core
    seqs = outer * inner
    split = seqs // H
    wide = DV // split
    blocks = []
    for n in range(2):
        rows = []
        for h in range(H):
            total = g_ref[h * split, n * DK : (n + 1) * DK, :]
            for s in range(1, split):
                total = total + g_ref[h * split + s, n * DK : (n + 1) * DK, :]
            rows.append(total)
        blocks.append(jnp.concatenate(rows, 0))
    for h in range(H):
        blocks.append(
            jnp.concatenate([g_ref[h * split + s, 2 * DK :, :] for s in range(split)], 0)
        )
    for i in range(pieces):
        for half in range(2):
            jb_ref[half, i] = blocks[half * pieces + i].astype(BF).astype(F32)
    gathers = []
    for i in range(pieces):
        row = []
        for k in range(1, plane):
            peer = (mine + k) % plane
            src = jb_ref.at[peer % 2, i]
            row.append(
                push(src, gj_ref.at[i, mine], send_j.at[i, k], recv_j.at[i, k], where(peer))
            )
        gathers.append(row)
    for n, block in enumerate(blocks):
        jt_ref[:, n * DV : (n + 1) * DV] = block.T.astype(BF)
    for i in range(pieces):
        gj_ref[i, mine] = jb_ref[core, i]
    for copy in loads:
        copy.wait()
    depth = gi_ref.shape[1] // pieces // 256 * 256
    starts = [i * depth for i in range(pieces)] + [gi_ref.shape[1]]
    tokens = plane * xb_ref.shape[1]
    rows = xb_ref.shape[2] // lines
    reduces = []
    for i in range(pieces):
        cut = slice(starts[i], starts[i + 1])
        total = dot(jt_ref[:, :DV], wq_ref[cut, :], (1, 1))
        total = total + dot(jt_ref[:, DV : 2 * DV], wk_ref[cut, :], (1, 1))
        total = total + dot(jt_ref[:, 2 * DV :], wv_ref[cut, :], (1, 1))
        gi_ref[:, cut] = total.astype(BF)
        for copy in gathers[i]:
            copy.wait_recv()
        grads = jnp.concatenate([gj_ref[i, j].astype(BF) for j in range(plane)], 1)
        part = dot(grads, xb_ref[...].reshape(tokens, xb_ref.shape[2]), (1, 0))
        for z in range(lines):
            ls_ref[i, z] = part[:, z * rows : (z + 1) * rows]
        row = []
        for k in range(1, lines):
            peer = (high + k) % lines
            row.append(
                push(ls_ref.at[i, peer], lr_ref.at[i, k], send_l.at[i, k], recv_l.at[i, k], along(peer))
            )
        reduces.append(row)
    lasts = []
    keep = rows // 2
    for i in range(pieces):
        total = ls_ref[i, high]
        for k, copy in enumerate(reduces[i]):
            copy.wait_recv()
            total = total + lr_ref[i, k + 1]
        fs_ref[i] = total.T
        src = fs_ref.at[i, pl.ds(pl.multiple_of(other * keep, keep), keep)]
        lasts.append(push(src, os_ref.at[i], send_o.at[i], recv_o.at[i], sibling(other)))
        o_ref[core * pieces + i] = fs_ref[i, pl.ds(pl.multiple_of(core * keep, keep), keep), :]
    for i, copy in enumerate(lasts):
        copy.wait_recv()
        o_ref[other * pieces + i] = os_ref[i]
    oq_ref[...] = o_ref[0]
    ok_ref[...] = o_ref[1]
    for n in range(H):
        ov_ref[:, n * DV : (n + 1) * DV] = o_ref[2 + n]
    for row in gathers + reduces + [lasts]:
        for copy in row:
            copy.wait_send()


def tail(grads, inside, weights, outer, inner):
    seqs, _, length = grads.shape
    width = weights[0].shape[0]
    pieces = sum(w.shape[1] for w in weights) // (2 * DV)
    rows = width // seqs
    plane = 2 * inner
    vm = lambda *shape: pltpu.VMEM(shape, F32)
    scratch = [pltpu.VMEM(w.shape, w.dtype) for w in weights] + [
        pltpu.VMEM((length, 2 * pieces * DV), BF),
        vm(2, pieces, DV, length),
        vm(pieces, plane, DV, length),
        vm(pieces, outer, DV, rows),
        vm(pieces, outer, DV, rows),
        vm(pieces, rows, DV),
        vm(pieces, rows // 2, DV),
        vm(2 * pieces, rows // 2, DV),
        sems(3),
        sems(pieces, plane), sems(pieces, plane),
        sems(pieces, outer), sems(pieces, outer),
        sems(pieces), sems(pieces),
    ]
    return pl.pallas_call(
        functools.partial(tail_kernel, outer, inner, pieces),
        out_shape=[
            jax.ShapeDtypeStruct((length, width), BF),
            jax.ShapeDtypeStruct((rows // 2, DV), F32),
            jax.ShapeDtypeStruct((rows // 2, DV), F32),
            jax.ShapeDtypeStruct((rows // 2, H * DV), F32),
        ],
        in_specs=[VMEM] * 2 + [HBM] * 3,
        out_specs=[VMEM] * 4,
        scratch_shapes=scratch,
        compiler_params=params(2),
    )(grads, inside, *weights)


def body(inputs, cotangent, w_query, w_key, w_value):
    seqs = lax.axis_size("seq")
    outer = 4 if seqs % 4 == 0 else 1
    inner = seqs // outer
    wide = DV * H // seqs
    tokens = inputs[0]
    weights = (w_query, w_key, w_value)
    received = front(tokens, cotangent[0], weights, outer, inner)
    grads, inside = attention(received, tokens, wide, outer, inner)
    grad_in, grad_wq, grad_wk, grad_wv = tail(grads, inside, weights, outer, inner)
    return (grad_in[None], grad_wq, grad_wk, grad_wv)


def solution(mesh):
    in_specs = (P("batch", "seq", None), P("batch", "seq", None), P(), P(), P())
    out_specs = (
        P("batch", "seq", None),
        P(("seq", "batch"), None),
        P(("seq", "batch"), None),
        P(("seq", "batch"), None),
    )
    return jax.shard_map(body, mesh=mesh, in_specs=in_specs, out_specs=out_specs, check_vma=False)
```

profile of v0, /device:TPU:93, one launch (start us, length us, event | category | flops | bytes accessed | tf_op | source)
XLA Modules:
  0.0 294.2 jit_solution(5758475799626363392)
XLA Ops:
  0.6 37.3 %shard_map.93.r_ref = f32[64,64,128]{2,1,0:T(8,128)} custom-call(bf16[128,2048]{1,0:T(8,128)(2,1)} %bitcast.3, bf16[128,1024]{1,0:T(8,128)(2,1)} %bitcast.6, bf16[2048,128]{1,0:T(8,128)(2,1)} %wq_hbm.3, bf16[2048,128]{1,0:T(8,128)(2,1)} %wk_hbm.3, bf16[2048,1024]{1,0:T(8,128)(2,1)} %wv_hbm.3), custom_call_target="tpu_custom_call" | custom-call | tf_op jit(solution)/shard_map/pallas_call | solution.py:338
  37.9 72.3 %shard_map.94 = (f32[64,48,128]{2,1,0:T(8,128)}, bf16[32,128,128]{2,1,0:T(8,128)(2,1)}) custom-call(f32[64,64,128]{2,1,0:T(8,128)} %shard_map.93.r_ref, f32[192,128]{1,0:T(8,128)} %constant.2.clone.c_ref, bf16[128,2048]{1,0:T(8,128)(2,1)} %bitcast.4), custom_call_target="tpu_custom_call" | custom-call | tf_op jit(solution)/shard_map/pallas_call | solution.py:273
  110.2 178.0 %shard_map.95 = (bf16[128,2048]{1,0:T(8,128)(2,1)}, f32[16,128]{1,0:T(8,128)}, f32[16,128]{1,0:T(8,128)}, f32[16,1024]{1,0:T(8,128)}) custom-call(f32[64,48,128]{2,1,0:T(8,128)} %get-tuple-element.10.g_ref, bf16[32,128,128]{2,1,0:T(8,128)(2,1)} %get-tuple-element.11.xb_ref, bf16[2048,128]{1,0:T(8,128)(2,1)} %wq_hbm.3, bf16[2048,128]{1,0:T(8,128)(2,1)} %wk_hbm.3, ...), custom_call_target="tpu_custom_call" | custom-call | tf_op jit(solution)/shard_map/pallas_call | solution.py:466
  288.2 1.9 copy.14
  290.1 1.3 copy.15
  291.4 1.3 copy.16
  292.7 1.5 copy.17
where the time goes:
time: 295 us; the launch traced here: 294 us
  Pallas kernels  288 us (98%)
  local copies, waits for them, and re-layouts  5.94 us (2%)
    pallas_call x1, Pallas kernels, tail(): pl.pallas_call(functools.partial(tail_kernel, outer, inner, pieces), out_...  178 us
    pallas_call x1, Pallas kernels, attention(): pl.pallas_call(functools.partial(attention_kernel, wide, outer, inner), o...  72.3 us
    pallas_call x1, Pallas kernels, front(): pl.pallas_call(functools.partial(front_kernel, outer, inner), out_shape=j...  37.3 us
    unnamed x4, local copies, waits for them, and re-layouts  5.94 us

commit v1 on v0

v1 whole, which is shorter than its diff:
```python
import functools
import math

import jax
import jax.numpy as jnp
from jax import lax
from jax.experimental import pallas as pl
from jax.experimental.pallas import tpu as pltpu
from jax.sharding import PartitionSpec as P

H = 8
DK = 16
DV = 128
F = 160
T = 128
N = 64
PART = F // 8
D = 2048
UNITS = 20
MESH = pl.DeviceIdType.MESH
BF = jnp.bfloat16
F32 = jnp.float32
ROOT = 1.0 / math.sqrt(2.0)
HBM = pl.BlockSpec(memory_space=pl.ANY)
VMEM = pl.BlockSpec(memory_space=pltpu.VMEM)


def dot(left, right, dims=(1, 0)):
    return lax.dot_general(left, right, ((dims[:1], dims[1:]), ((), ())), preferred_element_type=F32)


def halves(a):
    high = a.astype(BF)
    return high, (a - high.astype(F32)).astype(BF)


def dot2(pair, right, dims=(1, 0)):
    return dot(pair[0], right, dims) + dot(pair[1], right, dims)


def dot2r(left, pair, dims=(1, 0)):
    return dot(left, pair[0], dims) + dot(left, pair[1], dims)


def dot3(lefts, rights, dims=(1, 0)):
    return (
        dot(lefts[0], rights[0], dims)
        + dot(lefts[0], rights[1], dims)
        + dot(lefts[1], rights[0], dims)
    )


def ahead(a, d):
    return pltpu.roll(a, (8 - d) % 8, 0) if d % 8 else a


def back(a, d):
    return pltpu.roll(a, d, 0) if d % 8 else a


def phi(u):
    row = lax.broadcasted_iota(jnp.int32, (8, T), 0)
    low, high = u[:8], u[8:]
    tiles = []
    for m, fill in ((low, jnp.zeros((8, T), F32)), (high, (row == 4).astype(F32))):
        tiles.append(m * m * ROOT)
        for d in range(1, 4):
            tiles.append(m * ahead(m, d))
        tiles.append(jnp.where(row < 4, m * ahead(m, 4), fill))
    for d in range(8):
        tiles.append(low * ahead(high, d))
    return jnp.concatenate(tiles + [low, high], 0)


def pull(u, grad):
    row = lax.broadcasted_iota(jnp.int32, (8, T), 0)
    low, high = u[:8], u[8:]
    tile = lambda n: grad[8 * n : 8 * n + 8]
    sums = []
    for at, m in ((0, low), (5, high)):
        total = tile(18 + at // 5) + tile(at) * (2.0 * ROOT) * m
        for d in range(1, 5):
            piece = tile(at + d)
            if d == 4:
                piece = jnp.where(row < 4, piece, 0.0)
            total = total + piece * ahead(m, d) + back(piece * m, d)
        sums.append(total)
    for d in range(8):
        piece = tile(10 + d)
        sums[0] = sums[0] + piece * ahead(high, d)
        sums[1] = sums[1] + back(piece * low, d)
    return jnp.concatenate(sums, 0)


def kernel(
    x_hbm, c_hbm, wq_hbm, wk_hbm, wv_hbm, gi_ref, oq_ref, ok_ref, ov_ref,
    x_ref, c_ref, wq_ref, wk_ref, wv_ref,
    uq_ref, uk_ref, fqt, fkt, fqn, fkn, v_ref, ath, atl, ni_ref, rd_ref, gnh, gnl, ga_ref,
    gv_ref, gk_ref, sh_ref, gt_ref,
    s1, s2, s3, s4, t1, t2, t3, t4, nsrc, nrcv, tsrc, trcv,
    xt_ref, xr_ref, xp_ref, gs_ref, gr_ref, gp_ref,
    p_ref, a_ref, b_ref, q_ref, r2_ref, w_ref, r3_ref,
    load, a2s, a2r, lns, lnr, xs, xr, gss, grr, p1s, p1r, p2s, p2r, p3s, p3r,
):
    me = lax.axis_index("seq")
    core = lax.axis_index("batch")
    other = 1 - core
    at = (me // 16, (me // 4) % 4, me % 4)
    weight = (16, 4, 1)
    sends = []

    def along(d, c):
        return (me + (c - at[d]) * weight[d], core)

    def copy_to(src, dst, send, recv, device):
        return pltpu.make_async_remote_copy(
            src_ref=src, dst_ref=dst, send_sem=send, recv_sem=recv,
            device_id=device, device_id_type=MESH,
        )

    def push(src, dst, send, recv, device):
        copy = copy_to(src, dst, send, recv, device)
        copy.start()
        sends.append(copy)
        return copy

    loads = []
    for n, (src, dst) in enumerate(
        ((x_hbm, x_ref), (wk_hbm, wk_ref), (wq_hbm, wq_ref), (wv_hbm, wv_ref), (c_hbm, c_ref))
    ):
        copy = pltpu.make_async_copy(src, dst, load.at[n])
        copy.start()
        loads.append(copy)

    barrier = pltpu.get_barrier_semaphore()

    def greet(k, carry):
        pl.semaphore_signal(barrier, inc=1, device_id=((me + k) % N, core), device_id_type=MESH)
        return carry

    lax.fori_loop(1, N, greet, 0)
    pl.semaphore_signal(barrier, inc=1, device_id=(me, other), device_id_type=MESH)

    def scatter(src, dst, n):
        def step(k, carry):
            peer = (me + k) % N
            copy_to(src.at[peer], dst.at[me], a2s.at[n, peer], a2r.at[n, me], (peer, core)).start()
            return carry

        lax.fori_loop(1, N, step, 0)
        dst[me] = src[me]

    def arrive(dst, n, j):
        @pl.when(j != me)
        def _():
            copy_to(dst.at[j], dst.at[j], a2s.at[n, j], a2r.at[n, j], (j, core)).wait_recv()

    def sent(src, n):
        def step(k, carry):
            peer = (me + k) % N
            copy_to(src.at[peer], src.at[peer], a2s.at[n, peer], a2r.at[n, peer], (peer, core)).wait_send()
            return carry

        lax.fori_loop(1, N, step, 0)

    def scan(src, dst, n, reverse):
        def step(i, run):
            j = N - 1 - i if reverse else i
            arrive(src, n, j)
            dst[j] = run
            return run + src[j]

        lax.fori_loop(0, N, step, jnp.zeros((PART, DV), F32))

    def arrive_all(dst, n):
        def step(j, carry):
            arrive(dst, n, j)
            return carry

        lax.fori_loop(0, N, step, 0)

    def put_state(dst, h, value):
        for j in range(8):
            dst[8 * h + j, :16, :] = value[16 * j : 16 * j + 16]
            dst[8 * h + j, 16:, :] = value[128 + 4 * j : 132 + 4 * j]

    def get_state(src, h):
        tiles = [src[8 * h + j, :16, :] for j in range(8)]
        tiles += [src[8 * h + j, 16:, :] for j in range(8)]
        return jnp.concatenate(tiles, 0)

    def line_send(src, rcv, n, d):
        for k in range(1, 4):
            c = (at[d] + k) % 4
            push(src.at[d], rcv.at[d, at[d]], lns.at[n, d, k], lnr.at[n, d, at[d]], along(d, c))

    def line_sum(src, rcv, n, d, reverse):
        for k in range(1, 4):
            c = (at[d] + k) % 4
            copy_to(src.at[d], rcv.at[d, c], lns.at[n, d, k], lnr.at[n, d, c], along(d, c)).wait_recv()
        rcv[d, at[d]] = src[d]
        total = jnp.zeros((8, 256), F32)
        part = jnp.zeros((8, 256), F32)
        for c in range(4):
            block = rcv[d, c]
            total = total + block
            keep = c > at[d] if reverse else c < at[d]
            part = part + jnp.where(keep, block, 0.0)
        return total, part

    causal = lax.broadcasted_iota(jnp.int32, (T, T), 0) >= lax.broadcasted_iota(jnp.int32, (T, T), 1)
    anti = lax.broadcasted_iota(jnp.int32, (T, T), 0) <= lax.broadcasted_iota(jnp.int32, (T, T), 1)
    lane = lax.broadcasted_iota(jnp.int32, (T, DV), 1)
    ones = jnp.ones((T, DV), BF)
    rows8 = lax.broadcasted_iota(jnp.int32, (8, F), 0)

    loads[0].wait()
    loads[1].wait()
    x = x_ref[...]
    flat = dot(x, wk_ref[...]).T * 0.5
    norm = jnp.zeros((8, F), F32)
    for h in range(H):
        u = flat[DK * h : DK * h + DK]
        uk_ref[h] = u
        f = phi(u)
        ft = f.astype(BF)
        fkt[h] = ft
        fkn[h] = f.T.astype(BF)
        norm = jnp.where(rows8 == h, dot(jnp.ones((8, T), BF), ft, (1, 1)), norm)
    nsrc[2] = jnp.concatenate([norm, jnp.zeros((8, 256 - F), F32)], 1)
    pl.semaphore_wait(barrier, N)
    line_send(nsrc, nrcv, 0, 2)

    loads[3].wait()
    for h in range(H):
        val = dot(x, wv_ref[:, h * DV : (h + 1) * DV]).astype(BF)
        v_ref[h] = val
        put_state(s1, h, dot(fkt[h], val))
    scatter(s1, s2, 0)

    total, prefix = line_sum(nsrc, nrcv, 0, 2, False)
    nsrc[1] = total
    line_send(nsrc, nrcv, 0, 1)

    loads[2].wait()
    flat = dot(x, wq_ref[...]).T * 0.5
    for h in range(H):
        u = flat[DK * h : DK * h + DK]
        uq_ref[h] = u
        f = phi(u)
        fqt[h] = f.astype(BF)
        fqn[h] = f.T.astype(BF)

    total, part = line_sum(nsrc, nrcv, 0, 1, False)
    prefix = prefix + part
    nsrc[0] = total
    line_send(nsrc, nrcv, 0, 0)

    def inside(h):
        attn = halves(jnp.where(causal, dot(fqn[h], fkt[h]), 0.0))
        both = dot2(attn, jnp.concatenate([v_ref[h], ones], 1))
        ni_ref[h] = both[:, :DV]
        rd_ref[h] = both[:, DV:]
        turned = halves(jnp.where(anti, dot(fkn[h], fqt[h]), 0.0))
        ath[h] = turned[0]
        atl[h] = turned[1]

    for h in range(H):
        inside(h)
    total, part = line_sum(nsrc, nrcv, 0, 0, False)
    prefix = prefix + part
    loads[4].wait()

    for h in range(H):
        row = halves(jnp.broadcast_to(prefix[h : h + 1, :F], (DV, F)))
        den = rd_ref[h] + dot2r(fqn[h], row, (1, 1))
        scale = 1.0 / den
        rd_ref[h] = scale
        numer = c_ref[:, h * DV : (h + 1) * DV].astype(F32) * scale
        gn = halves(numer)
        gnh[h] = gn[0]
        gnl[h] = gn[1]
        put_state(t1, h, dot2r(fqt[h], gn))
    scatter(t1, t2, 2)

    for h in range(H):
        gn = (gnh[h], gnl[h])
        gv_ref[h] = dot3((ath[h], atl[h]), gn)
        ga_ref[h] = dot2(gn, v_ref[h], (1, 1))

    scan(s2, s3, 0, False)
    scatter(s3, s4, 1)

    for b in range(D // 128):
        block = x_ref[:, b * 128 : (b + 1) * 128].astype(F32).T
        for i in range(4):
            for half in range(2):
                row = 32 * i + 16 * half
                xt_ref[half, 4 * b + i] = block[row : row + 16]
    swap = push(xt_ref.at[other], xr_ref, xs.at[0], xr.at[0], (me, other))
    xp_ref[:, :T] = xt_ref[core].reshape(D // 2, T).astype(BF)

    scan(t2, t3, 2, True)
    scatter(t3, t4, 3)

    turned = jnp.concatenate([prefix, jnp.zeros((T - 8, 256), F32)], 0).T[:F]
    columns = halves(turned)
    arrive_all(s4, 1)
    down = jnp.zeros((F, DV), F32)
    grads = []
    for h in range(H):
        state = halves(get_state(s4, h))
        gn = (gnh[h], gnl[h])
        num = ni_ref[h] + dot2r(fqn[h], state)
        numer = gn[0].astype(F32) + gn[1].astype(F32)
        denom = -jnp.sum(numer * num, 1, keepdims=True) * rd_ref[h]
        ga = halves(jnp.where(causal, ga_ref[h] + denom, 0.0))
        mine = halves(jnp.where(lane == h, denom, 0.0))
        left = [jnp.concatenate([s, c], 1) for s, c in zip(state, columns)]
        right = [jnp.concatenate([g, m], 1) for g, m in zip(gn, mine)]
        gfq = dot2r(fkt[h], ga, (1, 1)) + dot3(left, right, (1, 1))
        grads.append(pull(uq_ref[h], gfq) * 0.5)
        gk_ref[h] = dot2r(fqt[h], ga)
        down = down + dot2r(fqt[h], mine)
    rows = jnp.concatenate([down, jnp.zeros((256 - F, DV), F32)], 0).T
    tsrc[2] = rows[:8]
    line_send(tsrc, trcv, 1, 2)
    grad_q = jnp.concatenate(grads, 0).T.astype(BF)

    def share(m, value):
        gp_ref[:T, 256 * m : 256 * m + 256] = value
        gs_ref[m] = value.astype(F32)
        return push(gs_ref.at[m], gr_ref.at[m], gss.at[m], grr.at[m], (me, other))

    arrive_all(t4, 3)
    shares = []
    for m in range(4):
        pieces = []
        for h in (2 * m, 2 * m + 1):
            state = halves(get_state(t4, h))
            sh_ref[h] = state[0]
            gt_ref[h] = state[1]
            pieces.append((gv_ref[h] + dot2r(fkn[h], state)).astype(BF))
        shares.append(share(m, jnp.concatenate(pieces, 1)))

    total, suffix = line_sum(tsrc, trcv, 1, 2, True)
    tsrc[1] = total
    line_send(tsrc, trcv, 1, 1)

    swap.wait_recv()
    xp_ref[:, T:] = xr_ref[...].reshape(D // 2, T).astype(BF)

    def multiply(m):
        shares[m].wait_recv()
        gp_ref[T:, 256 * m : 256 * m + 256] = gr_ref[m].astype(BF)
        right = gp_ref[:, 256 * m : 256 * m + 256]
        for z in range(4):
            part = dot(xp_ref[256 * z : 256 * z + 256, :], right)
            for i in range(2):
                block = part[:, i * DV : (i + 1) * DV].reshape(4, 4, 2, 8, DV)
                for r in range(2):
                    p_ref[4 * m + 2 * i + r, z] = block[:, :, r]

    def line_part(u, g, c, half):
        take = pl.ds(2 * half, 2)
        if g == 0:
            return (u, c, take)
        if g == 1:
            return (u, take, c)
        return (u, take, slice(None), c)

    first = {}

    def stage0(u):
        g = u % 3
        i = at[g]
        right, left, far = (i + 1) % 4, (i + 3) % 4, (i + 2) % 4
        keys = (
            (far, 0, right, a_ref.at[u, 0]),
            (far, 1, left, a_ref.at[u, 1]),
            (right, 1, right, b_ref.at[u, 0, pl.ds(2, 2)]),
            (left, 0, left, b_ref.at[u, 1, pl.ds(0, 2)]),
        )
        first[u] = [
            push(p_ref.at[line_part(u, g, c, half)], dst, p1s.at[u, n], p1r.at[u, n], along(g, peer))
            for n, (c, half, peer, dst) in enumerate(keys)
        ]

    def stage1(u):
        g = u % 3
        i = at[g]
        right, left = (i + 1) % 4, (i + 3) % 4
        for n, (peer, half) in enumerate(((right, 0), (left, 1))):
            first[u][n].wait_recv()
            where = line_part(u, g, peer, half)
            p_ref[where] = p_ref[where] + a_ref[u, n]
            dst = b_ref.at[u, n, pl.ds(2 * half, 2)]
            first[u].append(
                push(p_ref.at[where], dst, p1s.at[u, 4 + n], p1r.at[u, 4 + n], along(g, peer))
            )

    order = ((1, 2), (2, 0), (0, 1))

    def stage2(u):
        g = u % 3
        for n in range(2, 6):
            first[u][n].wait_recv()
        for half in range(2):
            mine = p_ref[line_part(u, g, at[g], half)]
            mine = mine + b_ref[u, 0, 2 * half : 2 * half + 2] + b_ref[u, 1, 2 * half : 2 * half + 2]
            for i in range(2):
                if g == 1:
                    q_ref[u, :, 2 * half + i] = mine[i]
                else:
                    q_ref[u, 2 * half + i] = mine[i]
        d = order[g][0]
        first[u] = []
        for k in range(1, 4):
            c = (at[d] + k) % 4
            first[u].append(
                push(q_ref.at[u, c], r2_ref.at[u, at[d]], p2s.at[u, k], p2r.at[u, at[d]], along(d, c))
            )

    def from_line(d, src, dst, send, recv, u):
        for k in range(1, 4):
            c = (at[d] + k) % 4
            copy_to(src.at[u, c], dst.at[u, c], send.at[u, k], recv.at[u, c], along(d, c)).wait_recv()
        total = src[u, at[d]]
        for k in range(1, 4):
            total = total + dst[u, (at[d] + k) % 4]
        return total

    def stage3(u):
        d, e = order[u % 3]
        w_ref[u] = from_line(d, q_ref, r2_ref, p2s, p2r, u)
        for k in range(1, 4):
            c = (at[e] + k) % 4
            push(w_ref.at[u, c], r3_ref.at[u, at[e]], p3s.at[u, k], p3r.at[u, at[e]], along(e, c))

    def stage4(u):
        total = from_line(order[u % 3][1], w_ref, r3_ref, p3s, p3r, u)
        piece, r = u // 2, u % 2
        rows = slice(8 * r, 8 * r + 8)
        if piece < H:
            ov_ref[rows, piece * DV : (piece + 1) * DV] = total
        else:
            (oq_ref if piece == H else ok_ref)[rows, :] = total

    multiply(0)
    for u in range(4):
        stage0(u)
    multiply(1)
    for u in range(4, 8):
        stage0(u)

    total, part = line_sum(tsrc, trcv, 1, 1, True)
    suffix = suffix + part
    tsrc[0] = total
    line_send(tsrc, trcv, 1, 0)

    multiply(2)
    for u in range(8, 12):
        stage0(u)
    multiply(3)
    for u in range(12, 16):
        stage0(u)
    for u in range(6):
        stage1(u)

    total, part = line_sum(tsrc, trcv, 1, 0, True)
    suffix = suffix + part
    turned = jnp.concatenate([suffix, jnp.zeros((T - 8, 256), F32)], 0).T[:F]
    grads = []
    for h in range(H):
        gfk = gk_ref[h] + dot2((sh_ref[h], gt_ref[h]), v_ref[h], (1, 1)) + turned[:, h : h + 1]
        grads.append(pull(uk_ref[h], gfk) * 0.5)
    grad_k = jnp.concatenate(grads, 0).T.astype(BF)
    shares.append(share(4, jnp.concatenate([grad_q, grad_k], 1)))
    for u in range(6, 12):
        stage1(u)
    multiply(4)
    for u in range(16, 20):
        stage0(u)
    for u in range(12, 16):
        stage1(u)

    wide = D // 8

    def inputs(n):
        cut = slice(n * wide, (n + 1) * wide)
        total = dot(gp_ref[:T, : H * DV], wv_ref[cut, :], (1, 1))
        total = total + dot(gp_ref[:T, H * DV : H * DV + 128], wq_ref[cut, :], (1, 1))
        total = total + dot(gp_ref[:T, H * DV + 128 :], wk_ref[cut, :], (1, 1))
        gi_ref[:, cut] = total.astype(BF)

    for n in range(2):
        inputs(n)
    for u in range(8):
        stage2(u)
    for n in range(2, 4):
        inputs(n)
    for u in range(16, 20):
        stage1(u)
    for n in range(4, 6):
        inputs(n)
    for u in range(8, 16):
        stage2(u)
    for u in range(8):
        stage3(u)
    for n in range(6, 8):
        inputs(n)
    for u in range(16, 20):
        stage2(u)
    for u in range(8, 16):
        stage3(u)
    for u in range(8):
        stage4(u)
    for u in range(16, 20):
        stage3(u)
    for u in range(8, 20):
        stage4(u)
    for copy in sends:
        copy.wait_send()
    for n, src in enumerate((s1, s3, t1, t3)):
        sent(src, n)


def body(inputs, cotangent, w_query, w_key, w_value):
    vm = lambda *shape: pltpu.VMEM(shape, F32)
    vb = lambda *shape: pltpu.VMEM(shape, BF)
    sems = lambda *sizes: pltpu.SemaphoreType.DMA(sizes)
    state = lambda: vm(N, PART, DV)
    scratch = [
        vb(T, D), vb(T, H * DV), vb(D, 128), vb(D, 128), vb(D, H * DV),
        vm(H, DK, T), vm(H, DK, T), vb(H, F, T), vb(H, F, T), vb(H, T, F), vb(H, T, F), vb(H, T, DV),
        vb(H, T, T), vb(H, T, T), vm(H, T, DV), vm(H, T, DV), vb(H, T, DV), vb(H, T, DV), vm(H, T, T),
        vm(H, T, DV), vm(H, F, T), vb(H, F, DV), vb(H, F, DV),
        state(), state(), state(), state(), state(), state(), state(), state(),
        vm(3, 8, 256), vm(3, 4, 8, 256), vm(3, 8, 256), vm(3, 4, 8, 256),
        vm(2, N, 16, T), vm(N, 16, T), vb(D // 2, 2 * T), vm(5, T, 256), vm(5, T, 256), vb(2 * T, 1280),
        vm(UNITS, 4, 4, 4, 8, DV), vm(UNITS, 2, 2, 4, 8, DV), vm(UNITS, 2, 4, 4, 8, DV),
        vm(UNITS, 4, 4, 8, DV), vm(UNITS, 4, 4, 8, DV), vm(UNITS, 4, 8, DV), vm(UNITS, 4, 8, DV),
        sems(5), sems(4, N), sems(4, N), sems(2, 3, 4), sems(2, 3, 4), sems(1), sems(1), sems(5), sems(5),
        sems(UNITS, 6), sems(UNITS, 6), sems(UNITS, 4), sems(UNITS, 4), sems(UNITS, 4), sems(UNITS, 4),
    ]
    grad_in, grad_wq, grad_wk, grad_wv = pl.pallas_call(
        kernel,
        out_shape=[
            jax.ShapeDtypeStruct((T, D), BF),
            jax.ShapeDtypeStruct((16, 128), F32),
            jax.ShapeDtypeStruct((16, 128), F32),
            jax.ShapeDtypeStruct((16, H * DV), F32),
        ],
        in_specs=[HBM] * 5,
        out_specs=[VMEM] * 4,
        scratch_shapes=scratch,
        compiler_params=pltpu.CompilerParams(
            collective_id=0, has_side_effects=True, vmem_limit_bytes=60 << 20
        ),
    )(inputs[0], cotangent[0], w_query, w_key, w_value)
    return (grad_in[None], grad_wq, grad_wk, grad_wv)


def solution(mesh):
    in_specs = (P("batch", "seq", None), P("batch", "seq", None), P(), P(), P())
    out_specs = (
        P("batch", "seq", None),
        P(("seq", "batch"), None),
        P(("seq", "batch"), None),
        P(("seq", "batch"), None),
    )
    return jax.shard_map(body, mesh=mesh, in_specs=in_specs, out_specs=out_specs, check_vma=False)
```

time: 295 us -> 106 us (0.36)
  the two profiles are of different devices: /device:TPU:93 before, /device:TPU:0 now
where the time goes in v1:
time: 106 us
  Pallas kernels  99.6 us (94%)
  local copies, waits for them, and re-layouts  5.94 us (6%)
    pallas_call x1, Pallas kernels, body(): pl.pallas_call(kernel, out_shape=[jax.ShapeDtypeStruct((T, D), BF), jax.S...  99.6 us
    unnamed x4, local copies, waits for them, and re-layouts  5.94 us

profile of v1, /device:TPU:0, one launch (start us, length us, event | category | flops | bytes accessed | tf_op | source)
XLA Modules:
  0.0 106.2 jit_solution(4959341536189198346)
XLA Ops:
  0.6 99.6 %shard_map.84 = (bf16[128,2048]{1,0:T(8,128)(2,1)}, f32[16,128]{1,0:T(8,128)}, f32[16,128]{1,0:T(8,128)}, f32[16,1024]{1,0:T(8,128)}) custom-call(bf16[128,2048]{1,0:T(8,128)(2,1)} %bitcast.3, bf16[128,1024]{1,0:T(8,128)(2,1)} %bitcast.5, bf16[2048,128]{1,0:T(8,128)(2,1)} %wq_hbm.1, bf16[2048,128]{1,0:T(8,128)(2,1)} %wk_hbm.1, bf16[2048,1024]{1,0:T(8,128)(2,1)} %wv_hbm.1), custom_call_target="tpu_custom_call" | custom-call | tf_op jit(solution)/shard_map/pallas_call | solution.py:546
  100.2 1.9 %copy.13 = bf16[1,128,2048]{2,1,0:T(8,128)(2,1)} copy(bf16[1,128,2048]{2,1,0:T(8,128)(2,1)} %bitcast.4) | data formatting | bytes 1048576
  102.1 1.3 %copy.14 = f32[16,128]{1,0:T(8,128)} copy(f32[16,128]{1,0:T(8,128)} %get-tuple-element.17) | data formatting | bytes 16384
  103.4 1.3 %copy.15 = f32[16,128]{1,0:T(8,128)} copy(f32[16,128]{1,0:T(8,128)} %get-tuple-element.18) | data formatting | bytes 16384
  104.7 1.5 %copy.16 = f32[16,1024]{1,0:T(8,128)} copy(f32[16,1024]{1,0:T(8,128)} %get-tuple-element.19) | data formatting | bytes 131072

commit v2 on v1

--- a/solution.py
+++ b/solution.py
@@ -93,7 +93,7 @@
 
 
 def kernel(
-    x_hbm, c_hbm, wq_hbm, wk_hbm, wv_hbm, gi_ref, oq_ref, ok_ref, ov_ref,
+    x_hbm, c_hbm, wq_hbm, wk_hbm, wv_hbm, gi_ref, o_ref,
     x_ref, c_ref, wq_ref, wk_ref, wv_ref,
     uq_ref, uk_ref, fqt, fkt, fqn, fkn, v_ref, ath, atl, ni_ref, rd_ref, gnh, gnl, ga_ref,
     gv_ref, gk_ref, sh_ref, gt_ref,
@@ -107,7 +107,6 @@
     other = 1 - core
     at = (me // 16, (me // 4) % 4, me % 4)
     weight = (16, 4, 1)
-    sends = []
 
     def along(d, c):
         return (me + (c - at[d]) * weight[d], core)
@@ -121,8 +120,10 @@
     def push(src, dst, send, recv, device):
         copy = copy_to(src, dst, send, recv, device)
         copy.start()
-        sends.append(copy)
         return copy
+
+    def drain(ref, sem):
+        copy_to(ref, ref, sem, sem, (me, other)).wait_send()
 
     loads = []
     for n, (src, dst) in enumerate(
@@ -144,7 +145,7 @@
     def scatter(src, dst, n):
         def step(k, carry):
             peer = (me + k) % N
-            copy_to(src.at[peer], dst.at[me], a2s.at[n, peer], a2r.at[n, me], (peer, core)).start()
+            copy_to(src.at[peer], dst.at[me], a2s.at[n], a2r.at[n, me], (peer, core)).start()
             return carry
 
         lax.fori_loop(1, N, step, 0)
@@ -153,15 +154,7 @@
     def arrive(dst, n, j):
         @pl.when(j != me)
         def _():
-            copy_to(dst.at[j], dst.at[j], a2s.at[n, j], a2r.at[n, j], (j, core)).wait_recv()
-
-    def sent(src, n):
-        def step(k, carry):
-            peer = (me + k) % N
-            copy_to(src.at[peer], src.at[peer], a2s.at[n, peer], a2r.at[n, peer], (peer, core)).wait_send()
-            return carry
-
-        lax.fori_loop(1, N, step, 0)
+            copy_to(dst.at[j], dst.at[j], a2s.at[n], a2r.at[n, j], (j, core)).wait_recv()
 
     def scan(src, dst, n, reverse):
         def step(i, run):
@@ -192,12 +185,11 @@
     def line_send(src, rcv, n, d):
         for k in range(1, 4):
             c = (at[d] + k) % 4
-            push(src.at[d], rcv.at[d, at[d]], lns.at[n, d, k], lnr.at[n, d, at[d]], along(d, c))
+            push(src.at[d], rcv.at[d, at[d]], lns.at[n, d], lnr.at[n, d], along(d, c))
 
     def line_sum(src, rcv, n, d, reverse):
-        for k in range(1, 4):
-            c = (at[d] + k) % 4
-            copy_to(src.at[d], rcv.at[d, c], lns.at[n, d, k], lnr.at[n, d, c], along(d, c)).wait_recv()
+        block = rcv.at[d, pl.ds(0, 3)]
+        copy_to(block, block, lns.at[n, d], lnr.at[n, d], (me, other)).wait_recv()
         rcv[d, at[d]] = src[d]
         total = jnp.zeros((8, 256), F32)
         part = jnp.zeros((8, 256), F32)
@@ -236,7 +228,6 @@
         val = dot(x, wv_ref[:, h * DV : (h + 1) * DV]).astype(BF)
         v_ref[h] = val
         put_state(s1, h, dot(fkt[h], val))
-    scatter(s1, s2, 0)
 
     total, prefix = line_sum(nsrc, nrcv, 0, 2, False)
     nsrc[1] = total
@@ -255,6 +246,7 @@
     prefix = prefix + part
     nsrc[0] = total
     line_send(nsrc, nrcv, 0, 0)
+    scatter(s1, s2, 0)
 
     def inside(h):
         attn = halves(jnp.where(causal, dot(fqn[h], fkt[h]), 0.0))
@@ -330,7 +322,7 @@
     def share(m, value):
         gp_ref[:T, 256 * m : 256 * m + 256] = value
         gs_ref[m] = value.astype(F32)
-        return push(gs_ref.at[m], gr_ref.at[m], gss.at[m], grr.at[m], (me, other))
+        return push(gs_ref.at[m], gr_ref.at[m], gss.at[0], grr.at[m], (me, other))
 
     arrive_all(t4, 3)
     shares = []
@@ -369,7 +361,8 @@
             return (u, take, c)
         return (u, take, slice(None), c)
 
-    first = {}
+    def arrived(ref, sem):
+        copy_to(ref, ref, sem, sem, (me, other)).wait_recv()
 
     def stage0(u):
         g = u % 3
@@ -381,30 +374,25 @@
             (right, 1, right, b_ref.at[u, 0, pl.ds(2, 2)]),
             (left, 0, left, b_ref.at[u, 1, pl.ds(0, 2)]),
         )
-        first[u] = [
-            push(p_ref.at[line_part(u, g, c, half)], dst, p1s.at[u, n], p1r.at[u, n], along(g, peer))
-            for n, (c, half, peer, dst) in enumerate(keys)
-        ]
+        for n, (c, half, peer, dst) in enumerate(keys):
+            push(p_ref.at[line_part(u, g, c, half)], dst, p1s.at[0], p1r.at[u, n // 2], along(g, peer))
 
     def stage1(u):
         g = u % 3
         i = at[g]
         right, left = (i + 1) % 4, (i + 3) % 4
+        arrived(a_ref.at[u], p1r.at[u, 0])
         for n, (peer, half) in enumerate(((right, 0), (left, 1))):
-            first[u][n].wait_recv()
             where = line_part(u, g, peer, half)
             p_ref[where] = p_ref[where] + a_ref[u, n]
             dst = b_ref.at[u, n, pl.ds(2 * half, 2)]
-            first[u].append(
-                push(p_ref.at[where], dst, p1s.at[u, 4 + n], p1r.at[u, 4 + n], along(g, peer))
-            )
+            push(p_ref.at[where], dst, p1s.at[1], p1r.at[u, 1], along(g, peer))
 
     order = ((1, 2), (2, 0), (0, 1))
 
     def stage2(u):
         g = u % 3
-        for n in range(2, 6):
-            first[u][n].wait_recv()
+        arrived(b_ref.at[u], p1r.at[u, 1])
         for half in range(2):
             mine = p_ref[line_part(u, g, at[g], half)]
             mine = mine + b_ref[u, 0, 2 * half : 2 * half + 2] + b_ref[u, 1, 2 * half : 2 * half + 2]
@@ -414,17 +402,12 @@
                 else:
                     q_ref[u, 2 * half + i] = mine[i]
         d = order[g][0]
-        first[u] = []
         for k in range(1, 4):
             c = (at[d] + k) % 4
-            first[u].append(
-                push(q_ref.at[u, c], r2_ref.at[u, at[d]], p2s.at[u, k], p2r.at[u, at[d]], along(d, c))
-            )
-
-    def from_line(d, src, dst, send, recv, u):
-        for k in range(1, 4):
-            c = (at[d] + k) % 4
-            copy_to(src.at[u, c], dst.at[u, c], send.at[u, k], recv.at[u, c], along(d, c)).wait_recv()
+            push(q_ref.at[u, c], r2_ref.at[u, at[d]], p2s.at[0], p2r.at[u], along(d, c))
+
+    def from_line(d, src, dst, recv, u):
+        arrived(dst.at[u, pl.ds(0, 3)], recv.at[u])
         total = src[u, at[d]]
         for k in range(1, 4):
             total = total + dst[u, (at[d] + k) % 4]
@@ -432,19 +415,16 @@
 
     def stage3(u):
         d, e = order[u % 3]
-        w_ref[u] = from_line(d, q_ref, r2_ref, p2s, p2r, u)
+        w_ref[u] = from_line(d, q_ref, r2_ref, p2r, u)
         for k in range(1, 4):
             c = (at[e] + k) % 4
-            push(w_ref.at[u, c], r3_ref.at[u, at[e]], p3s.at[u, k], p3r.at[u, at[e]], along(e, c))
+            push(w_ref.at[u, c], r3_ref.at[u, at[e]], p3s.at[0], p3r.at[u], along(e, c))
 
     def stage4(u):
-        total = from_line(order[u % 3][1], w_ref, r3_ref, p3s, p3r, u)
+        total = from_line(order[u % 3][1], w_ref, r3_ref, p3r, u)
         piece, r = u // 2, u % 2
         rows = slice(8 * r, 8 * r + 8)
-        if piece < H:
-            ov_ref[rows, piece * DV : (piece + 1) * DV] = total
-        else:
-            (oq_ref if piece == H else ok_ref)[rows, :] = total
+        o_ref[rows, piece * DV : (piece + 1) * DV] = total
 
     multiply(0)
     for u in range(4):
@@ -519,10 +499,39 @@
         stage3(u)
     for u in range(8, 20):
         stage4(u)
-    for copy in sends:
-        copy.wait_send()
     for n, src in enumerate((s1, s3, t1, t3)):
-        sent(src, n)
+        drain(src.at[pl.ds(0, N - 1)], a2s.at[n])
+    for n, rcv in enumerate((nrcv, trcv)):
+        for d in range(3):
+            drain(rcv.at[d, pl.ds(0, 3)], lns.at[n, d])
+    drain(xr_ref, xs.at[0])
+    drain(gr_ref, gss.at[0])
+    drain(b_ref, p1s.at[0])
+    drain(a_ref, p1s.at[1])
+    drain(q_ref.at[:, pl.ds(0, 3)], p2s.at[0])
+    drain(w_ref.at[:, pl.ds(0, 3)], p3s.at[0])
+
+
+def results(gi_in, w_in, gi_ref, oq_ref, ok_ref, ov_ref, g_ref, w_ref, load, save):
+    reads = [
+        pltpu.make_async_copy(gi_in, g_ref, load.at[0]),
+        pltpu.make_async_copy(w_in, w_ref, load.at[1]),
+    ]
+    for copy in reads:
+        copy.start()
+    reads[1].wait()
+    writes = [
+        pltpu.make_async_copy(w_ref.at[:, pl.ds(0, H * DV)], ov_ref, save.at[0]),
+        pltpu.make_async_copy(w_ref.at[:, pl.ds(H * DV, 128)], oq_ref, save.at[1]),
+        pltpu.make_async_copy(w_ref.at[:, pl.ds(H * DV + 128, 128)], ok_ref, save.at[2]),
+    ]
+    for copy in writes:
+        copy.start()
+    reads[0].wait()
+    writes.append(pltpu.make_async_copy(g_ref, gi_ref, save.at[3]))
+    writes[3].start()
+    for copy in writes:
+        copy.wait()
 
 
 def body(inputs, cotangent, w_query, w_key, w_value):
@@ -540,24 +549,31 @@
         vm(2, N, 16, T), vm(N, 16, T), vb(D // 2, 2 * T), vm(5, T, 256), vm(5, T, 256), vb(2 * T, 1280),
         vm(UNITS, 4, 4, 4, 8, DV), vm(UNITS, 2, 2, 4, 8, DV), vm(UNITS, 2, 4, 4, 8, DV),
         vm(UNITS, 4, 4, 8, DV), vm(UNITS, 4, 4, 8, DV), vm(UNITS, 4, 8, DV), vm(UNITS, 4, 8, DV),
-        sems(5), sems(4, N), sems(4, N), sems(2, 3, 4), sems(2, 3, 4), sems(1), sems(1), sems(5), sems(5),
-        sems(UNITS, 6), sems(UNITS, 6), sems(UNITS, 4), sems(UNITS, 4), sems(UNITS, 4), sems(UNITS, 4),
+        sems(5), sems(4), sems(4, N), sems(2, 3), sems(2, 3), sems(1), sems(1), sems(1), sems(5),
+        sems(2), sems(UNITS, 2), sems(1), sems(UNITS), sems(1), sems(UNITS),
     ]
+    grad_in, grad_w = pl.pallas_call(
+        kernel,
+        out_shape=[jax.ShapeDtypeStruct((T, D), BF), jax.ShapeDtypeStruct((16, 1280), F32)],
+        in_specs=[HBM] * 5,
+        out_specs=[VMEM] * 2,
+        scratch_shapes=scratch,
+        compiler_params=pltpu.CompilerParams(
+            collective_id=0, has_side_effects=True, vmem_limit_bytes=60 << 20
+        ),
+    )(inputs[0], cotangent[0], w_query, w_key, w_value)
     grad_in, grad_wq, grad_wk, grad_wv = pl.pallas_call(
-        kernel,
+        results,
         out_shape=[
             jax.ShapeDtypeStruct((T, D), BF),
             jax.ShapeDtypeStruct((16, 128), F32),
             jax.ShapeDtypeStruct((16, 128), F32),
             jax.ShapeDtypeStruct((16, H * DV), F32),
         ],
-        in_specs=[HBM] * 5,
-        out_specs=[VMEM] * 4,
-        scratch_shapes=scratch,
-        compiler_params=pltpu.CompilerParams(
-            collective_id=0, has_side_effects=True, vmem_limit_bytes=60 << 20
-        ),
-    )(inputs[0], cotangent[0], w_query, w_key, w_value)
+        in_specs=[HBM] * 2,
+        out_specs=[HBM] * 4,
+        scratch_shapes=[vb(T, D), vm(16, 1280), sems(2), sems(4)],
+    )(grad_in, grad_w)
     return (grad_in[None], grad_wq, grad_wk, grad_wv)
 
 

time: 106 us -> 90.5 us (0.85)
  Pallas kernels: 99.6 us -> 89 us
  local copies, waits for them, and re-layouts: 5.94 us -> 0 us
    pallas_call x1, Pallas kernels: 99.6 us -> 87.1 us  [body(): pl.pallas_call(kernel, out_shape=[jax.ShapeDtypeStruct((T, D), BF), jax.S...]
    unnamed x4 -> x0, local copies, waits for them, and re-layouts: 5.94 us -> none
    pallas_call x0 -> x1, Pallas kernels: none -> 1.92 us  [body(): pl.pallas_call(results, out_shape=[jax.ShapeDtypeStruct((T, D), BF), jax....]
where the time goes in v2:
time: 90.5 us; the launch traced here: 89.8 us
  Pallas kernels  89 us (98%)
    pallas_call x1, Pallas kernels, body(): pl.pallas_call(kernel, out_shape=[jax.ShapeDtypeStruct((T, D), BF), jax.S...  87.1 us
    pallas_call x1, Pallas kernels, body(): pl.pallas_call(results, out_shape=[jax.ShapeDtypeStruct((T, D), BF), jax....  1.92 us

profile of v2, /device:TPU:0, one launch (start us, length us, event | category | flops | bytes accessed | tf_op | source)
XLA Modules:
  0.0 89.8 jit_solution(9269676920332737763)
XLA Ops:
  0.6 87.1 %shard_map.84 = (bf16[128,2048]{1,0:T(8,128)(2,1)}, f32[16,1280]{1,0:T(8,128)}) custom-call(bf16[128,2048]{1,0:T(8,128)(2,1)} %bitcast.3, bf16[128,1024]{1,0:T(8,128)(2,1)} %bitcast.4, bf16[2048,128]{1,0:T(8,128)(2,1)} %wq_hbm.1, bf16[2048,128]{1,0:T(8,128)(2,1)} %wk_hbm.1, bf16[2048,1024]{1,0:T(8,128)(2,1)} %wv_hbm.1), custom_call_target="tpu_custom_call" | custom-call | tf_op jit(solution)/shard_map/pallas_call | solution.py:555
  87.7 1.9 %shard_map.85 = (bf16[128,2048]{1,0:T(8,128)(2,1)}, f32[16,128]{1,0:T(8,128)}, f32[16,128]{1,0:T(8,128)}, f32[16,1024]{1,0:T(8,128)}) custom-call(bf16[128,2048]{1,0:T(8,128)(2,1)} %get-tuple-element.10.gi_in, f32[16,1280]{1,0:T(8,128)} %get-tuple-element.11.w_in), custom_call_target="tpu_custom_call" | custom-call | tf_op jit(solution)/shard_map/pallas_call | solution.py:565

commit v3 on v2

--- a/solution.py
+++ b/solution.py
@@ -23,6 +23,12 @@
 ROOT = 1.0 / math.sqrt(2.0)
 HBM = pl.BlockSpec(memory_space=pl.ANY)
 VMEM = pl.BlockSpec(memory_space=pltpu.VMEM)
+
+
+OFFSETS = sorted(
+    ((a, b, c) for a in range(4) for b in range(4) for c in range(4) if a + b + c),
+    key=lambda o: -sum(min(v, 4 - v) for v in o),
+)
 
 
 def dot(left, right, dims=(1, 0)):
@@ -142,13 +148,13 @@
     lax.fori_loop(1, N, greet, 0)
     pl.semaphore_signal(barrier, inc=1, device_id=(me, other), device_id_type=MESH)
 
+    def peers():
+        part = [[(at[d] + k) % 4 * weight[d] for k in range(4)] for d in range(3)]
+        return [part[0][a] + part[1][b] + part[2][c] for a, b, c in OFFSETS]
+
     def scatter(src, dst, n):
-        def step(k, carry):
-            peer = (me + k) % N
+        for peer in peers():
             copy_to(src.at[peer], dst.at[me], a2s.at[n], a2r.at[n, me], (peer, core)).start()
-            return carry
-
-        lax.fori_loop(1, N, step, 0)
         dst[me] = src[me]
 
     def arrive(dst, n, j):
@@ -182,35 +188,42 @@
         tiles += [src[8 * h + j, 16:, :] for j in range(8)]
         return jnp.concatenate(tiles, 0)
 
-    def line_send(src, rcv, n, d):
-        for k in range(1, 4):
-            c = (at[d] + k) % 4
-            push(src.at[d], rcv.at[d, at[d]], lns.at[n, d], lnr.at[n, d], along(d, c))
-
-    def line_sum(src, rcv, n, d, reverse):
-        block = rcv.at[d, pl.ds(0, 3)]
-        copy_to(block, block, lns.at[n, d], lnr.at[n, d], (me, other)).wait_recv()
-        rcv[d, at[d]] = src[d]
-        total = jnp.zeros((8, 256), F32)
-        part = jnp.zeros((8, 256), F32)
-        for c in range(4):
-            block = rcv[d, c]
-            total = total + block
-            keep = c > at[d] if reverse else c < at[d]
-            part = part + jnp.where(keep, block, 0.0)
-        return total, part
+    def gather(src, rcv, n):
+        for peer in peers():
+            copy_to(src, rcv.at[me], lns.at[n], lnr.at[n], (peer, core)).start()
+        rcv[me] = src[...]
+
+    def gathered(rcv, n, low, high):
+        blocks = rcv.at[pl.ds(0, N - 1)]
+        copy_to(blocks, blocks, lns.at[n], lnr.at[n], (me, other)).wait_recv()
+
+        def step(j, total):
+            return total + rcv[j]
+
+        total = lax.fori_loop(low, high, step, jnp.zeros((10, DV), F32))
+        rows = []
+        for h in range(H):
+            at_lane = 32 * (h % 4)
+            rest = total[8 + h // 4 : 9 + h // 4, at_lane : at_lane + 32]
+            rows.append(jnp.concatenate([total[h : h + 1], rest], 1))
+        return jnp.concatenate(rows, 0)
+
+    def turn(rows):
+        wide = jnp.concatenate([rows, jnp.zeros((8, 256 - F), F32)], 1)
+        return jnp.concatenate([wide, jnp.zeros((T - 8, 256), F32)], 0).T[:F]
 
     causal = lax.broadcasted_iota(jnp.int32, (T, T), 0) >= lax.broadcasted_iota(jnp.int32, (T, T), 1)
     anti = lax.broadcasted_iota(jnp.int32, (T, T), 0) <= lax.broadcasted_iota(jnp.int32, (T, T), 1)
     lane = lax.broadcasted_iota(jnp.int32, (T, DV), 1)
     ones = jnp.ones((T, DV), BF)
-    rows8 = lax.broadcasted_iota(jnp.int32, (8, F), 0)
+    rows8 = lax.broadcasted_iota(jnp.int32, (8, DV), 0)
 
     loads[0].wait()
     loads[1].wait()
     x = x_ref[...]
     flat = dot(x, wk_ref[...]).T * 0.5
-    norm = jnp.zeros((8, F), F32)
+    norm = jnp.zeros((8, DV), F32)
+    one = jnp.ones((8, T), BF)
     for h in range(H):
         u = flat[DK * h : DK * h + DK]
         uk_ref[h] = u
@@ -218,21 +231,21 @@
         ft = f.astype(BF)
         fkt[h] = ft
         fkn[h] = f.T.astype(BF)
-        norm = jnp.where(rows8 == h, dot(jnp.ones((8, T), BF), ft, (1, 1)), norm)
-    nsrc[2] = jnp.concatenate([norm, jnp.zeros((8, 256 - F), F32)], 1)
+        norm = jnp.where(rows8 == h, dot(one, ft[:DV], (1, 1)), norm)
+    nsrc[:8] = norm
+    for i in range(2):
+        last = jnp.concatenate([fkt[h, DV:] for h in range(4 * i, 4 * i + 4)], 0)
+        nsrc[8 + i : 9 + i] = dot(one, last, (1, 1))[:1]
     pl.semaphore_wait(barrier, N)
-    line_send(nsrc, nrcv, 0, 2)
+    gather(nsrc, nrcv, 0)
 
     loads[3].wait()
-    for h in range(H):
-        val = dot(x, wv_ref[:, h * DV : (h + 1) * DV]).astype(BF)
-        v_ref[h] = val
-        put_state(s1, h, dot(fkt[h], val))
-
-    total, prefix = line_sum(nsrc, nrcv, 0, 2, False)
-    nsrc[1] = total
-    line_send(nsrc, nrcv, 0, 1)
-
+    for m in range(4):
+        both = dot(x, wv_ref[:, 256 * m : 256 * m + 256]).astype(BF)
+        for i in range(2):
+            val = both[:, i * DV : (i + 1) * DV]
+            v_ref[2 * m + i] = val
+            put_state(s1, 2 * m + i, dot(fkt[2 * m + i], val))
     loads[2].wait()
     flat = dot(x, wq_ref[...]).T * 0.5
     for h in range(H):
@@ -241,12 +254,6 @@
         f = phi(u)
         fqt[h] = f.astype(BF)
         fqn[h] = f.T.astype(BF)
-
-    total, part = line_sum(nsrc, nrcv, 0, 1, False)
-    prefix = prefix + part
-    nsrc[0] = total
-    line_send(nsrc, nrcv, 0, 0)
-    scatter(s1, s2, 0)
 
     def inside(h):
         attn = halves(jnp.where(causal, dot(fqn[h], fkt[h]), 0.0))
@@ -259,12 +266,12 @@
 
     for h in range(H):
         inside(h)
-    total, part = line_sum(nsrc, nrcv, 0, 0, False)
-    prefix = prefix + part
+    scatter(s1, s2, 0)
+    prefix = gathered(nrcv, 0, 0, me)
     loads[4].wait()
 
     for h in range(H):
-        row = halves(jnp.broadcast_to(prefix[h : h + 1, :F], (DV, F)))
+        row = halves(jnp.broadcast_to(prefix[h : h + 1], (DV, F)))
         den = rd_ref[h] + dot2r(fqn[h], row, (1, 1))
         scale = 1.0 / den
         rd_ref[h] = scale
@@ -295,7 +302,12 @@
     scan(t2, t3, 2, True)
     scatter(t3, t4, 3)
 
-    turned = jnp.concatenate([prefix, jnp.zeros((T - 8, 256), F32)], 0).T[:F]
+    def share(m, value):
+        gp_ref[:T, 256 * m : 256 * m + 256] = value
+        gs_ref[m] = value.astype(F32)
+        return push(gs_ref.at[m], gr_ref.at[m], gss.at[0], grr.at[m], (me, other))
+
+    turned = turn(prefix)
     columns = halves(turned)
     arrive_all(s4, 1)
     down = jnp.zeros((F, DV), F32)
@@ -315,14 +327,13 @@
         gk_ref[h] = dot2r(fqt[h], ga)
         down = down + dot2r(fqt[h], mine)
     rows = jnp.concatenate([down, jnp.zeros((256 - F, DV), F32)], 0).T
-    tsrc[2] = rows[:8]
-    line_send(tsrc, trcv, 1, 2)
+    tsrc[:8] = rows[:8, :DV]
+    for i in range(2):
+        tsrc[8 + i : 9 + i] = jnp.concatenate(
+            [rows[h : h + 1, DV:F] for h in range(4 * i, 4 * i + 4)], 1
+        )
+    gather(tsrc, trcv, 1)
     grad_q = jnp.concatenate(grads, 0).T.astype(BF)
-
-    def share(m, value):
-        gp_ref[:T, 256 * m : 256 * m + 256] = value
-        gs_ref[m] = value.astype(F32)
-        return push(gs_ref.at[m], gr_ref.at[m], gss.at[0], grr.at[m], (me, other))
 
     arrive_all(t4, 3)
     shares = []
@@ -334,10 +345,6 @@
             gt_ref[h] = state[1]
             pieces.append((gv_ref[h] + dot2r(fkn[h], state)).astype(BF))
         shares.append(share(m, jnp.concatenate(pieces, 1)))
-
-    total, suffix = line_sum(tsrc, trcv, 1, 2, True)
-    tsrc[1] = total
-    line_send(tsrc, trcv, 1, 1)
 
     swap.wait_recv()
     xp_ref[:, T:] = xr_ref[...].reshape(D // 2, T).astype(BF)
@@ -426,44 +433,22 @@
         rows = slice(8 * r, 8 * r + 8)
         o_ref[rows, piece * DV : (piece + 1) * DV] = total
 
-    multiply(0)
-    for u in range(4):
-        stage0(u)
-    multiply(1)
-    for u in range(4, 8):
-        stage0(u)
-
-    total, part = line_sum(tsrc, trcv, 1, 1, True)
-    suffix = suffix + part
-    tsrc[0] = total
-    line_send(tsrc, trcv, 1, 0)
-
-    multiply(2)
-    for u in range(8, 12):
-        stage0(u)
-    multiply(3)
-    for u in range(12, 16):
-        stage0(u)
-    for u in range(6):
-        stage1(u)
-
-    total, part = line_sum(tsrc, trcv, 1, 0, True)
-    suffix = suffix + part
-    turned = jnp.concatenate([suffix, jnp.zeros((T - 8, 256), F32)], 0).T[:F]
+    for m in range(2):
+        multiply(m)
+        for u in range(4 * m, 4 * m + 4):
+            stage0(u)
+    suffix = gathered(trcv, 1, me + 1, N)
+    turned = turn(suffix)
     grads = []
     for h in range(H):
         gfk = gk_ref[h] + dot2((sh_ref[h], gt_ref[h]), v_ref[h], (1, 1)) + turned[:, h : h + 1]
         grads.append(pull(uk_ref[h], gfk) * 0.5)
     grad_k = jnp.concatenate(grads, 0).T.astype(BF)
     shares.append(share(4, jnp.concatenate([grad_q, grad_k], 1)))
-    for u in range(6, 12):
-        stage1(u)
-    multiply(4)
-    for u in range(16, 20):
-        stage0(u)
-    for u in range(12, 16):
-        stage1(u)
-
+    for m in range(2, 5):
+        multiply(m)
+        for u in range(4 * m, 4 * m + 4):
+            stage0(u)
     wide = D // 8
 
     def inputs(n):
@@ -473,37 +458,30 @@
         total = total + dot(gp_ref[:T, H * DV + 128 :], wk_ref[cut, :], (1, 1))
         gi_ref[:, cut] = total.astype(BF)
 
-    for n in range(2):
+    for n in range(4):
         inputs(n)
     for u in range(8):
+        stage1(u)
+    for n in range(4, 8):
+        inputs(n)
+    for u in range(8, 20):
+        stage1(u)
+        if u >= 14:
+            stage2(u - 14)
+    for u in range(6, 20):
         stage2(u)
-    for n in range(2, 4):
-        inputs(n)
-    for u in range(16, 20):
-        stage1(u)
-    for n in range(4, 6):
-        inputs(n)
-    for u in range(8, 16):
-        stage2(u)
-    for u in range(8):
+        if u >= 12:
+            stage3(u - 12)
+    for u in range(8, 20):
         stage3(u)
-    for n in range(6, 8):
-        inputs(n)
-    for u in range(16, 20):
-        stage2(u)
-    for u in range(8, 16):
-        stage3(u)
-    for u in range(8):
-        stage4(u)
-    for u in range(16, 20):
-        stage3(u)
-    for u in range(8, 20):
+        if u >= 14:
+            stage4(u - 14)
+    for u in range(6, 20):
         stage4(u)
     for n, src in enumerate((s1, s3, t1, t3)):
         drain(src.at[pl.ds(0, N - 1)], a2s.at[n])
     for n, rcv in enumerate((nrcv, trcv)):
-        for d in range(3):
-            drain(rcv.at[d, pl.ds(0, 3)], lns.at[n, d])
+        drain(rcv.at[pl.ds(0, N - 1)], lns.at[n])
     drain(xr_ref, xs.at[0])
     drain(gr_ref, gss.at[0])
     drain(b_ref, p1s.at[0])
@@ -512,24 +490,15 @@
     drain(w_ref.at[:, pl.ds(0, 3)], p3s.at[0])
 
 
-def results(gi_in, w_in, gi_ref, oq_ref, ok_ref, ov_ref, g_ref, w_ref, load, save):
-    reads = [
-        pltpu.make_async_copy(gi_in, g_ref, load.at[0]),
-        pltpu.make_async_copy(w_in, w_ref, load.at[1]),
-    ]
-    for copy in reads:
-        copy.start()
-    reads[1].wait()
+def results(g_ref, w_ref, gi_ref, oq_ref, ok_ref, ov_ref, save):
     writes = [
-        pltpu.make_async_copy(w_ref.at[:, pl.ds(0, H * DV)], ov_ref, save.at[0]),
-        pltpu.make_async_copy(w_ref.at[:, pl.ds(H * DV, 128)], oq_ref, save.at[1]),
-        pltpu.make_async_copy(w_ref.at[:, pl.ds(H * DV + 128, 128)], ok_ref, save.at[2]),
+        pltpu.make_async_copy(g_ref, gi_ref, save.at[0]),
+        pltpu.make_async_copy(w_ref.at[:, pl.ds(0, H * DV)], ov_ref, save.at[1]),
+        pltpu.make_async_copy(w_ref.at[:, pl.ds(H * DV, 128)], oq_ref, save.at[2]),
+        pltpu.make_async_copy(w_ref.at[:, pl.ds(H * DV + 128, 128)], ok_ref, save.at[3]),
     ]
     for copy in writes:
         copy.start()
-    reads[0].wait()
-    writes.append(pltpu.make_async_copy(g_ref, gi_ref, save.at[3]))
-    writes[3].start()
     for copy in writes:
         copy.wait()
 
@@ -545,16 +514,16 @@
         vb(H, T, T), vb(H, T, T), vm(H, T, DV), vm(H, T, DV), vb(H, T, DV), vb(H, T, DV), vm(H, T, T),
         vm(H, T, DV), vm(H, F, T), vb(H, F, DV), vb(H, F, DV),
         state(), state(), state(), state(), state(), state(), state(), state(),
-        vm(3, 8, 256), vm(3, 4, 8, 256), vm(3, 8, 256), vm(3, 4, 8, 256),
+        vm(10, DV), vm(N, 10, DV), vm(10, DV), vm(N, 10, DV),
         vm(2, N, 16, T), vm(N, 16, T), vb(D // 2, 2 * T), vm(5, T, 256), vm(5, T, 256), vb(2 * T, 1280),
         vm(UNITS, 4, 4, 4, 8, DV), vm(UNITS, 2, 2, 4, 8, DV), vm(UNITS, 2, 4, 4, 8, DV),
         vm(UNITS, 4, 4, 8, DV), vm(UNITS, 4, 4, 8, DV), vm(UNITS, 4, 8, DV), vm(UNITS, 4, 8, DV),
-        sems(5), sems(4), sems(4, N), sems(2, 3), sems(2, 3), sems(1), sems(1), sems(1), sems(5),
+        sems(6), sems(4), sems(4, N), sems(2), sems(2), sems(1), sems(1), sems(1), sems(5),
         sems(2), sems(UNITS, 2), sems(1), sems(UNITS), sems(1), sems(UNITS),
     ]
     grad_in, grad_w = pl.pallas_call(
         kernel,
-        out_shape=[jax.ShapeDtypeStruct((T, D), BF), jax.ShapeDtypeStruct((16, 1280), F32)],
+        out_shape=[vb(T, D), vm(16, 1280)],
         in_specs=[HBM] * 5,
         out_specs=[VMEM] * 2,
         scratch_shapes=scratch,
@@ -570,10 +539,10 @@
             jax.ShapeDtypeStruct((16, 128), F32),
             jax.ShapeDtypeStruct((16, H * DV), F32),
         ],
-        in_specs=[HBM] * 2,
+        in_specs=[VMEM] * 2,
         out_specs=[HBM] * 4,
-        scratch_shapes=[vb(T, D), vm(16, 1280), sems(2), sems(4)],
-    )(grad_in, grad_w)
+        scratch_shapes=[sems(4)],
+    )(*(pltpu.with_memory_space_constraint(g, pltpu.VMEM) for g in (grad_in, grad_w)))
     return (grad_in[None], grad_wq, grad_wk, grad_wv)
 
 

time: 90.5 us -> 83.3 us (0.920)
  Pallas kernels: 89 us -> 82.4 us
    pallas_call x1, Pallas kernels: 87.1 us -> 81.6 us  [body(): pl.pallas_call(kernel, out_shape=[vb(T, D), vm(16, 1280)], in_specs=[HBM]...]
    pallas_call x1, Pallas kernels: 1.92 us -> 0.84 us  [body(): pl.pallas_call(results, out_shape=[jax.ShapeDtypeStruct((T, D), BF), jax....]
where the time goes in v3:
time: 83.3 us; the launch traced here: 83.2 us
  Pallas kernels  82.4 us (99%)
    pallas_call x1, Pallas kernels, body(): pl.pallas_call(kernel, out_shape=[vb(T, D), vm(16, 1280)], in_specs=[HBM]...  81.6 us

profile of v3, /device:TPU:0, one launch (start us, length us, event | category | flops | bytes accessed | tf_op | source)
XLA Modules:
  0.0 83.2 jit_solution(34291527386064363)
XLA Ops:
  0.6 81.6 %shard_map.84 = (bf16[128,2048]{1,0:T(8,128)(2,1)S(1)}, f32[16,1280]{1,0:T(8,128)S(1)}) custom-call(bf16[128,2048]{1,0:T(8,128)(2,1)} %bitcast.3, bf16[128,1024]{1,0:T(8,128)(2,1)} %bitcast.4, bf16[2048,128]{1,0:T(8,128)(2,1)} %wq_hbm.1, bf16[2048,128]{1,0:T(8,128)(2,1)} %wk_hbm.1, bf16[2048,1024]{1,0:T(8,128)(2,1)} %wv_hbm.1), custom_call_target="tpu_custom_call" | custom-call | tf_op jit(solution)/shard_map/pallas_call | solution.py:524
  82.2 0.8 %shard_map.85 = (bf16[128,2048]{1,0:T(8,128)(2,1)}, f32[16,128]{1,0:T(8,128)}, f32[16,128]{1,0:T(8,128)}, f32[16,1024]{1,0:T(8,128)}) custom-call(bf16[128,2048]{1,0:T(8,128)(2,1)S(1)} %get-tuple-element.10.g_ref, f32[16,1280]{1,0:T(8,128)S(1)} %get-tuple-element.11.w_ref), custom_call_target="tpu_custom_call" | custom-call | tf_op jit(solution)/shard_map/pallas_call | solution.py:534

commit v4 on v3

--- a/solution.py
+++ b/solution.py
@@ -17,6 +17,7 @@
 PART = F // 8
 D = 2048
 UNITS = 20
+LAST = 14
 MESH = pl.DeviceIdType.MESH
 BF = jnp.bfloat16
 F32 = jnp.float32
@@ -106,7 +107,7 @@
     s1, s2, s3, s4, t1, t2, t3, t4, nsrc, nrcv, tsrc, trcv,
     xt_ref, xr_ref, xp_ref, gs_ref, gr_ref, gp_ref,
     p_ref, a_ref, b_ref, q_ref, r2_ref, w_ref, r3_ref,
-    load, a2s, a2r, lns, lnr, xs, xr, gss, grr, p1s, p1r, p2s, p2r, p3s, p3r,
+    load, a2s, a2r, lns, lnr, xs, xr, gss, grr, p1s, p1r, p2s, p2r, p4s, p4r, r4_ref, p3s, p3r,
 ):
     me = lax.axis_index("seq")
     core = lax.axis_index("batch")
@@ -154,29 +155,24 @@
 
     def scatter(src, dst, n):
         for peer in peers():
-            copy_to(src.at[peer], dst.at[me], a2s.at[n], a2r.at[n, me], (peer, core)).start()
+            copy_to(src.at[peer], dst.at[me], a2s.at[n], a2r.at[n], (peer, core)).start()
         dst[me] = src[me]
 
-    def arrive(dst, n, j):
-        @pl.when(j != me)
-        def _():
-            copy_to(dst.at[j], dst.at[j], a2s.at[n], a2r.at[n, j], (j, core)).wait_recv()
+    def arrive_all(dst, n):
+        blocks = dst.at[pl.ds(0, N - 1)]
+        copy_to(blocks, blocks, a2s.at[n], a2r.at[n], (me, other)).wait_recv()
 
     def scan(src, dst, n, reverse):
+        arrive_all(src, n)
+
         def step(i, run):
-            j = N - 1 - i if reverse else i
-            arrive(src, n, j)
-            dst[j] = run
-            return run + src[j]
-
-        lax.fori_loop(0, N, step, jnp.zeros((PART, DV), F32))
-
-    def arrive_all(dst, n):
-        def step(j, carry):
-            arrive(dst, n, j)
-            return carry
-
-        lax.fori_loop(0, N, step, 0)
+            for k in range(8):
+                j = N - 1 - 8 * i - k if reverse else 8 * i + k
+                dst[j] = run
+                run = run + src[j]
+            return run
+
+        lax.fori_loop(0, N // 8, step, jnp.zeros((PART, DV), F32))
 
     def put_state(dst, h, value):
         for j in range(8):
@@ -368,8 +364,10 @@
             return (u, take, c)
         return (u, take, slice(None), c)
 
-    def arrived(ref, sem):
-        copy_to(ref, ref, sem, sem, (me, other)).wait_recv()
+    def arrived(ref, sem, u, more=()):
+        if u % 2 == 0:
+            pair = ref.at[(pl.ds(u, 2),) + more]
+            copy_to(pair, pair, sem, sem, (me, other)).wait_recv()
 
     def stage0(u):
         g = u % 3
@@ -382,24 +380,24 @@
             (left, 0, left, b_ref.at[u, 1, pl.ds(0, 2)]),
         )
         for n, (c, half, peer, dst) in enumerate(keys):
-            push(p_ref.at[line_part(u, g, c, half)], dst, p1s.at[0], p1r.at[u, n // 2], along(g, peer))
+            push(p_ref.at[line_part(u, g, c, half)], dst, p1s.at[0], p1r.at[u // 2, n // 2], along(g, peer))
 
     def stage1(u):
         g = u % 3
         i = at[g]
         right, left = (i + 1) % 4, (i + 3) % 4
-        arrived(a_ref.at[u], p1r.at[u, 0])
+        arrived(a_ref, p1r.at[u // 2, 0], u)
         for n, (peer, half) in enumerate(((right, 0), (left, 1))):
             where = line_part(u, g, peer, half)
             p_ref[where] = p_ref[where] + a_ref[u, n]
             dst = b_ref.at[u, n, pl.ds(2 * half, 2)]
-            push(p_ref.at[where], dst, p1s.at[1], p1r.at[u, 1], along(g, peer))
+            push(p_ref.at[where], dst, p1s.at[1], p1r.at[u // 2, 1], along(g, peer))
 
     order = ((1, 2), (2, 0), (0, 1))
 
     def stage2(u):
         g = u % 3
-        arrived(b_ref.at[u], p1r.at[u, 1])
+        arrived(b_ref, p1r.at[u // 2, 1], u)
         for half in range(2):
             mine = p_ref[line_part(u, g, at[g], half)]
             mine = mine + b_ref[u, 0, 2 * half : 2 * half + 2] + b_ref[u, 1, 2 * half : 2 * half + 2]
@@ -408,27 +406,45 @@
                     q_ref[u, :, 2 * half + i] = mine[i]
                 else:
                     q_ref[u, 2 * half + i] = mine[i]
-        d = order[g][0]
+        d, e = order[g]
+        if u >= LAST:
+            for k in range(1, 16):
+                a, b = (at[d] + k // 4) % 4, (at[e] + k % 4) % 4
+                peer = me + (a - at[d]) * weight[d] + (b - at[e]) * weight[e]
+                dst = r4_ref.at[u - LAST, 4 * at[d] + at[e]]
+                push(q_ref.at[u, a, b], dst, p4s.at[0], p4r.at[u // 2 - LAST // 2], (peer, core))
+            return
         for k in range(1, 4):
             c = (at[d] + k) % 4
-            push(q_ref.at[u, c], r2_ref.at[u, at[d]], p2s.at[0], p2r.at[u], along(d, c))
+            push(q_ref.at[u, c], r2_ref.at[u, at[d]], p2s.at[0], p2r.at[u // 2], along(d, c))
 
     def from_line(d, src, dst, recv, u):
-        arrived(dst.at[u, pl.ds(0, 3)], recv.at[u])
+        arrived(dst, recv.at[u // 2], u, (pl.ds(0, 3),))
         total = src[u, at[d]]
         for k in range(1, 4):
             total = total + dst[u, (at[d] + k) % 4]
         return total
 
     def stage3(u):
+        if u >= LAST:
+            return
         d, e = order[u % 3]
         w_ref[u] = from_line(d, q_ref, r2_ref, p2r, u)
         for k in range(1, 4):
             c = (at[e] + k) % 4
-            push(w_ref.at[u, c], r3_ref.at[u, at[e]], p3s.at[0], p3r.at[u], along(e, c))
+            push(w_ref.at[u, c], r3_ref.at[u, at[e]], p3s.at[0], p3r.at[u // 2], along(e, c))
 
     def stage4(u):
-        total = from_line(order[u % 3][1], w_ref, r3_ref, p3r, u)
+        if u < LAST:
+            total = from_line(order[u % 3][1], w_ref, r3_ref, p3r, u)
+        else:
+            n = u - LAST
+            arrived(r4_ref, p4r.at[n // 2], n, (pl.ds(0, 15),))
+            d, e = order[u % 3]
+            r4_ref[n, 4 * at[d] + at[e]] = q_ref[u, at[d], at[e]]
+            total = r4_ref[n, 0]
+            for k in range(1, 16):
+                total = total + r4_ref[n, k]
         piece, r = u // 2, u % 2
         rows = slice(8 * r, 8 * r + 8)
         o_ref[rows, piece * DV : (piece + 1) * DV] = total
@@ -486,8 +502,9 @@
     drain(gr_ref, gss.at[0])
     drain(b_ref, p1s.at[0])
     drain(a_ref, p1s.at[1])
-    drain(q_ref.at[:, pl.ds(0, 3)], p2s.at[0])
-    drain(w_ref.at[:, pl.ds(0, 3)], p3s.at[0])
+    drain(q_ref.at[pl.ds(0, LAST), pl.ds(0, 3)], p2s.at[0])
+    drain(w_ref.at[pl.ds(0, LAST), pl.ds(0, 3)], p3s.at[0])
+    drain(r4_ref.at[:, pl.ds(0, 15)], p4s.at[0])
 
 
 def results(g_ref, w_ref, gi_ref, oq_ref, ok_ref, ov_ref, save):
@@ -518,8 +535,8 @@
         vm(2, N, 16, T), vm(N, 16, T), vb(D // 2, 2 * T), vm(5, T, 256), vm(5, T, 256), vb(2 * T, 1280),
         vm(UNITS, 4, 4, 4, 8, DV), vm(UNITS, 2, 2, 4, 8, DV), vm(UNITS, 2, 4, 4, 8, DV),
         vm(UNITS, 4, 4, 8, DV), vm(UNITS, 4, 4, 8, DV), vm(UNITS, 4, 8, DV), vm(UNITS, 4, 8, DV),
-        sems(6), sems(4), sems(4, N), sems(2), sems(2), sems(1), sems(1), sems(1), sems(5),
-        sems(2), sems(UNITS, 2), sems(1), sems(UNITS), sems(1), sems(UNITS),
+        sems(5), sems(4), sems(4), sems(2), sems(2), sems(1), sems(1), sems(1), sems(5),
+        sems(2), sems(UNITS // 2, 2), sems(1), sems(UNITS // 2), sems(1), sems(3), vm(UNITS - LAST, 16, 8, DV), sems(1), sems(UNITS // 2),
     ]
     grad_in, grad_w = pl.pallas_call(
         kernel,

time: 83.3 us -> 79 us (0.948)
  Pallas kernels: 82.4 us -> 78.1 us
    pallas_call x1, Pallas kernels: 81.6 us -> 77.2 us  [body(): pl.pallas_call(kernel, out_shape=[vb(T, D), vm(16, 1280)], in_specs=[HBM]...]
where the time goes in v4:
time: 79 us; the launch traced here: 78.9 us
  Pallas kernels  78.1 us (99%)
  between operations  0.8 us (1%)
    pallas_call x1, Pallas kernels, body(): pl.pallas_call(kernel, out_shape=[vb(T, D), vm(16, 1280)], in_specs=[HBM]...  77.2 us

profile of v4, /device:TPU:0, one launch (start us, length us, event | category | flops | bytes accessed | tf_op | source)
XLA Modules:
  0.0 78.9 jit_solution(1299276010171102904)
XLA Ops:
  0.6 77.2 %shard_map.84 = (bf16[128,2048]{1,0:T(8,128)(2,1)S(1)}, f32[16,1280]{1,0:T(8,128)S(1)}) custom-call(bf16[128,2048]{1,0:T(8,128)(2,1)} %bitcast.3, bf16[128,1024]{1,0:T(8,128)(2,1)} %bitcast.4, bf16[2048,128]{1,0:T(8,128)(2,1)} %wq_hbm.1, bf16[2048,128]{1,0:T(8,128)(2,1)} %wk_hbm.1, bf16[2048,1024]{1,0:T(8,128)(2,1)} %wv_hbm.1), custom_call_target="tpu_custom_call" | custom-call | tf_op jit(solution)/shard_map/pallas_call | solution.py:541
  77.9 0.8 %shard_map.85 = (bf16[128,2048]{1,0:T(8,128)(2,1)}, f32[16,128]{1,0:T(8,128)}, f32[16,128]{1,0:T(8,128)}, f32[16,1024]{1,0:T(8,128)}) custom-call(bf16[128,2048]{1,0:T(8,128)(2,1)S(1)} %get-tuple-element.10.g_ref, f32[16,1280]{1,0:T(8,128)S(1)} %get-tuple-element.11.w_ref), custom_call_target="tpu_custom_call" | custom-call | tf_op jit(solution)/shard_map/pallas_call | solution.py:551

commit v5 on v4

--- a/solution.py
+++ b/solution.py
@@ -132,6 +132,15 @@
     def drain(ref, sem):
         copy_to(ref, ref, sem, sem, (me, other)).wait_send()
 
+    def peers():
+        part = [[(at[d] + k) % 4 * weight[d] for k in range(4)] for d in range(3)]
+        return [part[0][a] + part[1][b] + part[2][c] for a, b, c in OFFSETS]
+
+    barrier = pltpu.get_barrier_semaphore()
+    for peer in peers():
+        pl.semaphore_signal(barrier, inc=1, device_id=(peer, core), device_id_type=MESH)
+    pl.semaphore_signal(barrier, inc=1, device_id=(me, other), device_id_type=MESH)
+
     loads = []
     for n, (src, dst) in enumerate(
         ((x_hbm, x_ref), (wk_hbm, wk_ref), (wq_hbm, wq_ref), (wv_hbm, wv_ref), (c_hbm, c_ref))
@@ -139,19 +148,6 @@
         copy = pltpu.make_async_copy(src, dst, load.at[n])
         copy.start()
         loads.append(copy)
-
-    barrier = pltpu.get_barrier_semaphore()
-
-    def greet(k, carry):
-        pl.semaphore_signal(barrier, inc=1, device_id=((me + k) % N, core), device_id_type=MESH)
-        return carry
-
-    lax.fori_loop(1, N, greet, 0)
-    pl.semaphore_signal(barrier, inc=1, device_id=(me, other), device_id_type=MESH)
-
-    def peers():
-        part = [[(at[d] + k) % 4 * weight[d] for k in range(4)] for d in range(3)]
-        return [part[0][a] + part[1][b] + part[2][c] for a, b, c in OFFSETS]
 
     def scatter(src, dst, n):
         for peer in peers():
@@ -449,10 +445,12 @@
         rows = slice(8 * r, 8 * r + 8)
         o_ref[rows, piece * DV : (piece + 1) * DV] = total
 
-    for m in range(2):
+    for m in range(4):
         multiply(m)
         for u in range(4 * m, 4 * m + 4):
             stage0(u)
+    for u in range(4):
+        stage1(u)
     suffix = gathered(trcv, 1, me + 1, N)
     turned = turn(suffix)
     grads = []
@@ -461,7 +459,7 @@
         grads.append(pull(uk_ref[h], gfk) * 0.5)
     grad_k = jnp.concatenate(grads, 0).T.astype(BF)
     shares.append(share(4, jnp.concatenate([grad_q, grad_k], 1)))
-    for m in range(2, 5):
+    for m in range(4, 5):
         multiply(m)
         for u in range(4 * m, 4 * m + 4):
             stage0(u)
@@ -476,7 +474,7 @@
 
     for n in range(4):
         inputs(n)
-    for u in range(8):
+    for u in range(4, 8):
         stage1(u)
     for n in range(4, 8):
         inputs(n)

time: 79 us -> 76.5 us (0.968)
  Pallas kernels: 78.1 us -> 75.4 us
    pallas_call x1, Pallas kernels: 77.2 us -> 74.6 us  [body(): pl.pallas_call(kernel, out_shape=[vb(T, D), vm(16, 1280)], in_specs=[HBM]...]
where the time goes in v5:
time: 76.5 us; the launch traced here: 76.2 us
  Pallas kernels  75.4 us (99%)
  between operations  0.8 us (1%)
    pallas_call x1, Pallas kernels, body(): pl.pallas_call(kernel, out_shape=[vb(T, D), vm(16, 1280)], in_specs=[HBM]...  74.6 us

profile of v5, /device:TPU:0, one launch (start us, length us, event | category | flops | bytes accessed | tf_op | source)
XLA Modules:
  0.0 76.2 jit_solution(10581125643363310071)
XLA Ops:
  0.6 74.6 %shard_map.84 = (bf16[128,2048]{1,0:T(8,128)(2,1)S(1)}, f32[16,1280]{1,0:T(8,128)S(1)}) custom-call(bf16[128,2048]{1,0:T(8,128)(2,1)} %bitcast.3, bf16[128,1024]{1,0:T(8,128)(2,1)} %bitcast.4, bf16[2048,128]{1,0:T(8,128)(2,1)} %wq_hbm.1, bf16[2048,128]{1,0:T(8,128)(2,1)} %wk_hbm.1, bf16[2048,1024]{1,0:T(8,128)(2,1)} %wv_hbm.1), custom_call_target="tpu_custom_call" | custom-call | tf_op jit(solution)/shard_map/pallas_call | solution.py:539
  75.2 0.8 %shard_map.85 = (bf16[128,2048]{1,0:T(8,128)(2,1)}, f32[16,128]{1,0:T(8,128)}, f32[16,128]{1,0:T(8,128)}, f32[16,1024]{1,0:T(8,128)}) custom-call(bf16[128,2048]{1,0:T(8,128)(2,1)S(1)} %get-tuple-element.10.g_ref, f32[16,1280]{1,0:T(8,128)S(1)} %get-tuple-element.11.w_ref), custom_call_target="tpu_custom_call" | custom-call | tf_op jit(solution)/shard_map/pallas_call | solution.py:549

commit v6 on v5

--- a/solution.py
+++ b/solution.py
@@ -17,7 +17,7 @@
 PART = F // 8
 D = 2048
 UNITS = 20
-LAST = 14
+LAST = 16
 MESH = pl.DeviceIdType.MESH
 BF = jnp.bfloat16
 F32 = jnp.float32
@@ -534,7 +534,7 @@
         vm(UNITS, 4, 4, 4, 8, DV), vm(UNITS, 2, 2, 4, 8, DV), vm(UNITS, 2, 4, 4, 8, DV),
         vm(UNITS, 4, 4, 8, DV), vm(UNITS, 4, 4, 8, DV), vm(UNITS, 4, 8, DV), vm(UNITS, 4, 8, DV),
         sems(5), sems(4), sems(4), sems(2), sems(2), sems(1), sems(1), sems(1), sems(5),
-        sems(2), sems(UNITS // 2, 2), sems(1), sems(UNITS // 2), sems(1), sems(3), vm(UNITS - LAST, 16, 8, DV), sems(1), sems(UNITS // 2),
+        sems(2), sems(UNITS // 2, 2), sems(1), sems(UNITS // 2), sems(1), sems(2), vm(UNITS - LAST, 16, 8, DV), sems(1), sems(UNITS // 2),
     ]
     grad_in, grad_w = pl.pallas_call(
         kernel,

time: 76.5 us -> 77.6 us (1.014)
  Pallas kernels: 75.4 us -> 76.7 us
    pallas_call x1, Pallas kernels: 74.6 us -> 75.9 us  [body(): pl.pallas_call(kernel, out_shape=[vb(T, D), vm(16, 1280)], in_specs=[HBM]...]
where the time goes in v6:
time: 77.6 us; the launch traced here: 77.5 us
  Pallas kernels  76.7 us (99%)
  between operations  0.8 us (1%)
    pallas_call x1, Pallas kernels, body(): pl.pallas_call(kernel, out_shape=[vb(T, D), vm(16, 1280)], in_specs=[HBM]...  75.9 us

profile of v6, /device:TPU:0, one launch (start us, length us, event | category | flops | bytes accessed | tf_op | source)
XLA Modules:
  0.0 77.5 jit_solution(15927413843449895471)
XLA Ops:
  0.6 75.9 %shard_map.84 = (bf16[128,2048]{1,0:T(8,128)(2,1)S(1)}, f32[16,1280]{1,0:T(8,128)S(1)}) custom-call(bf16[128,2048]{1,0:T(8,128)(2,1)} %bitcast.3, bf16[128,1024]{1,0:T(8,128)(2,1)} %bitcast.4, bf16[2048,128]{1,0:T(8,128)(2,1)} %wq_hbm.1, bf16[2048,128]{1,0:T(8,128)(2,1)} %wk_hbm.1, bf16[2048,1024]{1,0:T(8,128)(2,1)} %wv_hbm.1), custom_call_target="tpu_custom_call" | custom-call | tf_op jit(solution)/shard_map/pallas_call | solution.py:539
  76.5 0.8 %shard_map.85 = (bf16[128,2048]{1,0:T(8,128)(2,1)}, f32[16,128]{1,0:T(8,128)}, f32[16,128]{1,0:T(8,128)}, f32[16,1024]{1,0:T(8,128)}) custom-call(bf16[128,2048]{1,0:T(8,128)(2,1)S(1)} %get-tuple-element.10.g_ref, f32[16,1280]{1,0:T(8,128)S(1)} %get-tuple-element.11.w_ref), custom_call_target="tpu_custom_call" | custom-call | tf_op jit(solution)/shard_map/pallas_call | solution.py:549
